TPU v7x, 64 devices: a 2x2x8 block of a 4x4x8 slice. The times are simulated.
64 devices in a mesh: data: 4 (over x, y), seq: 16 (over z, core).
Axes of the slice: x: 2, y: 2, z: 8, core: 2. Of those that a mesh axis runs over, the one named last changes fastest.
The devices are a block of a 4x4x8 slice.
Arguments:
- dec_in: bfloat16 [8192, 768], P(('data', 'seq')), parts along dimension 0
- memory: bfloat16 [65536, 768], P(('data', 'seq')), parts along dimension 0
- mem_len: int32 [4], P('data'), parts along dimension 0
- grad_out: float32 [8192, 768], P(('data', 'seq')), parts along dimension 0
- norm_attn: bfloat16 [768], replicated
- wq_cross: bfloat16 [768, 12, 64], replicated
- wk_cross: bfloat16 [768, 12, 64], replicated
- wv_cross: bfloat16 [768, 12, 64], replicated
- wo_cross: bfloat16 [12, 64, 768], replicated
- norm_mlp: bfloat16 [768], replicated
- w_gate: bfloat16 [768, 2048], replicated
- w_up: bfloat16 [768, 2048], replicated
- w_down: bfloat16 [2048, 768], replicated
Outputs:
- output 1: float32 [8192, 768], P(('data', 'seq')), parts along dimension 0
- output 2: float32 [65536, 768], P(('data', 'seq')), parts along dimension 0
- output 3: float32 [3072], P('data'), parts along dimension 0
- output 4: float32 [3072, 12, 64], P('data'), parts along dimension 0
- output 5: float32 [3072, 12, 64], P('data'), parts along dimension 0
- output 6: float32 [3072, 12, 64], P('data'), parts along dimension 0
- output 7: float32 [48, 64, 768], P('data'), parts along dimension 0
- output 8: float32 [3072], P('data'), parts along dimension 0
- output 9: float32 [3072, 2048], P('data'), parts along dimension 0
- output 10: float32 [3072, 2048], P('data'), parts along dimension 0
- output 11: float32 [8192, 768], P('data'), parts along dimension 0
There are 4 independent parts. A program takes and returns all parts, laid end to end along the dimension named above; an argument that names none is the same for every part.
All inputs are finite; a program needn't handle non-finite values.
Results may differ from a plain program's by a relative error of at most 0.0157877.
Values are sent between devices in bfloat16 or wider.
A program may use at most 768 MiB of HBM per device.

v0:
```python
import jax
import jax.numpy as jnp
from jax import lax
from jax.sharding import PartitionSpec as P


def rms_norm(tensor, gain):
    mean_sq = jnp.mean(tensor * tensor, axis=-1, keepdims=True)
    return tensor * lax.rsqrt(mean_sq + 1e-6) * gain


def gated_unit(gate_pre, up_pre):
    return jax.nn.silu(gate_pre) * up_pre


def solution(mesh):
    group_size = mesh.shape['seq']
    row_spec = P(('data', 'seq'), None)
    weight_spec = P()
    part_vec = P('data')
    part_mat = P('data', None)
    part_cube = P('data', None, None)

    def device_step(dec_in, memory, mem_len, grad_out, norm_attn, wq_cross, wk_cross, wv_cross, wo_cross, norm_mlp, w_gate, w_up, w_down):
        q_rows, model_dim = dec_in.shape
        m_rows = memory.shape[0]
        heads, head_dim = wq_cross.shape[1], wq_cross.shape[2]
        kv_heads = wk_cross.shape[1]
        head_group = heads // kv_heads
        score_scale = head_dim ** -0.5
        wo_grouped = wo_cross.reshape(kv_heads, head_group, head_dim, model_dim)
        mem_pos = lax.axis_index('seq') * m_rows + jnp.arange(m_rows)
        valid_mask = mem_pos < mem_len[0]

        x_in = dec_in.astype(jnp.float32)
        normed_f, norm_pull = jax.vjp(rms_norm, x_in, norm_attn.astype(jnp.float32))
        normed = normed_f.astype(jnp.bfloat16)
        local_query = jnp.einsum('td,dhe->the', normed, wq_cross, preferred_element_type=jnp.float32).astype(jnp.bfloat16)
        dec_query = lax.all_gather(local_query, 'seq', axis=0, tiled=True).reshape(q_rows * group_size, kv_heads, head_group, head_dim)
        mem_keys = jnp.einsum('td,dke->tke', memory, wk_cross, preferred_element_type=jnp.float32).astype(jnp.bfloat16)
        mem_vals = jnp.einsum('td,dke->tke', memory, wv_cross, preferred_element_type=jnp.float32).astype(jnp.bfloat16)

        def masked_scores():
            raw_scores = jnp.einsum('qkge,tke->kqgt', dec_query, mem_keys, preferred_element_type=jnp.float32)
            return jnp.where(valid_mask, raw_scores * score_scale, -1e30)

        scores = masked_scores()
        local_max = jnp.max(scores, axis=-1)
        exp_scores = jnp.exp(scores - local_max[..., None])
        local_sum = jnp.sum(exp_scores, axis=-1)
        local_out = jnp.einsum('kqgt,tke->kqge', exp_scores.astype(jnp.bfloat16), mem_vals, preferred_element_type=jnp.float32)
        global_max = lax.pmax(local_max, 'seq')
        rescale = jnp.exp(local_max - global_max)
        out_sum = lax.psum_scatter(local_out * rescale[..., None], 'seq', scatter_dimension=1, tiled=True)
        den_sum = lax.psum_scatter(local_sum * rescale, 'seq', scatter_dimension=1, tiled=True)
        attended_f = out_sum / den_sum[..., None]
        attended = attended_f.astype(jnp.bfloat16)
        hidden_f = x_in + jnp.einsum('kqge,kged->qd', attended, wo_grouped, preferred_element_type=jnp.float32)
        hidden = hidden_f.astype(jnp.bfloat16)
        normed_mlp_f, mlp_norm_pull = jax.vjp(rms_norm, hidden.astype(jnp.float32), norm_mlp.astype(jnp.float32))
        normed_mlp = normed_mlp_f.astype(jnp.bfloat16)
        gate_pre = jnp.dot(normed_mlp, w_gate, preferred_element_type=jnp.float32)
        up_pre = jnp.dot(normed_mlp, w_up, preferred_element_type=jnp.float32)
        mlp_f, gated_pull = jax.vjp(gated_unit, gate_pre, up_pre)
        mlp_act = mlp_f.astype(jnp.bfloat16)

        grad_top = grad_out.astype(jnp.bfloat16)
        g_down = jnp.einsum('qf,qd->fd', mlp_act, grad_top, preferred_element_type=jnp.float32)
        grad_act = jnp.einsum('qd,fd->qf', grad_top, w_down, preferred_element_type=jnp.float32)
        grad_gate, grad_up = gated_pull(grad_act)
        grad_gate_b = grad_gate.astype(jnp.bfloat16)
        grad_up_b = grad_up.astype(jnp.bfloat16)
        g_gate = jnp.einsum('qd,qf->df', normed_mlp, grad_gate_b, preferred_element_type=jnp.float32)
        g_up = jnp.einsum('qd,qf->df', normed_mlp, grad_up_b, preferred_element_type=jnp.float32)
        grad_normed_mlp = (jnp.einsum('qf,df->qd', grad_gate_b, w_gate, preferred_element_type=jnp.float32)
                           + jnp.einsum('qf,df->qd', grad_up_b, w_up, preferred_element_type=jnp.float32))
        grad_hidden_norm, g_norm_mlp = mlp_norm_pull(grad_normed_mlp)
        grad_hidden = grad_out + grad_hidden_norm
        grad_hidden_b = grad_hidden.astype(jnp.bfloat16)
        g_wo = jnp.einsum('kqge,qd->kged', attended, grad_hidden_b, preferred_element_type=jnp.float32).reshape(heads, head_dim, model_dim)
        grad_attended = jnp.einsum('qd,kged->kqge', grad_hidden_b, wo_grouped, preferred_element_type=jnp.float32)
        row_delta = jnp.sum(grad_attended * attended_f, axis=-1)
        grad_att_all = lax.all_gather(grad_attended.astype(jnp.bfloat16), 'seq', axis=1, tiled=True)
        stats = lax.all_gather(jnp.stack([den_sum, row_delta]), 'seq', axis=2, tiled=True)
        attn_prob = jnp.exp(masked_scores() - global_max[..., None]) / stats[0][..., None]
        grad_prob = jnp.einsum('kqge,tke->kqgt', grad_att_all, mem_vals, preferred_element_type=jnp.float32)
        grad_scores = (attn_prob * (grad_prob - stats[1][..., None]) * score_scale).astype(jnp.bfloat16)
        grad_vals = jnp.einsum('kqgt,kqge->tke', attn_prob.astype(jnp.bfloat16), grad_att_all, preferred_element_type=jnp.float32)
        grad_keys = jnp.einsum('kqgt,qkge->tke', grad_scores, dec_query, preferred_element_type=jnp.float32)
        grad_query_part = jnp.einsum('kqgt,tke->kqge', grad_scores, mem_keys, preferred_element_type=jnp.float32)
        grad_query = lax.psum_scatter(grad_query_part, 'seq', scatter_dimension=1, tiled=True)
        grad_query_b = jnp.transpose(grad_query, (1, 0, 2, 3)).reshape(q_rows, heads, head_dim).astype(jnp.bfloat16)
        g_wq = jnp.einsum('td,the->dhe', normed, grad_query_b, preferred_element_type=jnp.float32)
        grad_normed = jnp.einsum('the,dhe->td', grad_query_b, wq_cross, preferred_element_type=jnp.float32)
        grad_x_norm, g_norm_attn = norm_pull(grad_normed)
        g_dec = grad_hidden + grad_x_norm
        grad_keys_b = grad_keys.astype(jnp.bfloat16)
        grad_vals_b = grad_vals.astype(jnp.bfloat16)
        g_wk = jnp.einsum('td,tke->dke', memory, grad_keys_b, preferred_element_type=jnp.float32)
        g_wv = jnp.einsum('td,tke->dke', memory, grad_vals_b, preferred_element_type=jnp.float32)
        g_mem = (jnp.einsum('tke,dke->td', grad_keys_b, wk_cross, preferred_element_type=jnp.float32)
                 + jnp.einsum('tke,dke->td', grad_vals_b, wv_cross, preferred_element_type=jnp.float32))
        weight_grads = lax.psum((g_norm_attn, g_wq, g_wk, g_wv, g_wo, g_norm_mlp, g_gate, g_up, g_down), 'seq')
        return (g_dec, g_mem) + tuple(weight_grads)

    return jax.shard_map(device_step, mesh=mesh,
                         in_specs=(row_spec, row_spec, part_vec, row_spec) + (weight_spec,) * 9,
                         out_specs=(row_spec, row_spec, part_vec, part_cube, part_cube, part_cube, part_cube, part_vec, part_mat, part_mat, part_mat),
                         check_vma=False)
```

profile of v0, /device:TPU:21, one launch (start us, length us, event | category | flops | bytes accessed | tf_op | source)
XLA Modules:
  0.0 874.7 jit_solution(7251827327141830196)
XLA Ops:
  13.3 5.0 fusion.72
  21.4 37.5 %all-gather.3.cloned.1.call-done = bf16[2048,12,64]{0,2,1:T(8,128)(2,1)} async-done(((bf16[128,12,64]{0,2,1:T(8,128)(2,1)}), bf16[2048,12,64]{0,2,1:T(8,128)(2,1)}) %all-gather.3.cloned.1.call-update) | async-done | bytes 3145744 | tf_op jit(solution)/shard_map/all_gather | solution.py:39
  58.8 37.1 %fusion.2 = (f32[12,2048]{1,0:T(8,128)}, f32[12,2048,1024]{1,2,0:T(8,128)}) fusion(pred[1024]{0:T(1024)(128)(4,1)S(1)} %add_compare_fusion, bf16[2048,12,64]{0,2,1:T(8,128)(2,1)} %all-gather.3.cloned.1.call-done, f32[1024,12,64]{0,2,1:T(8,128)} %bitcast.126), kind=kOutput, calls=%fused_computation.6 | convolution fusion | flops 3297484800 | bytes 107054080 | tf_op jit(solution)/shard_map/qkge,tke->kqgt/dot_general | solution.py:44
  96.1 31.4 %fusion = f32[12,2048]{1,0:T(8,128)S(1)} fusion(f32[12,2048,1024]{1,2,0:T(8,128)} %get-tuple-element.33, f32[12,2048]{1,0:T(8,128)} %get-tuple-element.32, pred[1024]{0:T(1024)(128)(4,1)S(1)} %add_compare_fusion), kind=kLoop, calls=%fused_computation.4 | loop fusion | flops 100638720 | bytes 100860928 | tf_op jit(solution)/shard_map/reduce_sum | solution.py:50
  127.4 70.6 %all-reduce.5.cloned.1.call-done = f32[12,2048,1]{1,0,2:T(8,128)} async-done(((f32[12,2048,1]{1,0,2:T(8,128)}), f32[12,2048,1]{1,0,2:T(8,128)}) %all-reduce.5.cloned.1.call-update) | async-done | bytes 98320 | tf_op jit(solution)/shard_map/pmax | solution.py:52
  199.7 37.0 %multiply_bitcast_fusion = f32[12,2048,1,64]{1,3,0,2:T(8,128)} fusion(f32[12,2048,1024]{1,2,0:T(8,128)} %get-tuple-element.33, f32[12,2048]{1,0:T(8,128)S(1)} %copy-done.18, pred[1024]{0:T(1024)(128)(4,1)S(1)} %add_compare_fusion, f32[12,2048]{1,0:T(8,128)S(1)} %get-tuple-element.31, f32[1024,12,64]{0,2,1:T(8,128)} %bitcast.148), kind=kOutput, calls=%fused_computation.11 | convolution fusion | flops 3324248064 | bytes 110298112 | tf_op jit(solution)/shard_map/kqgt,tke->kqge/dot_general | solution.py:51
  237.4 15.0 %reduce-scatter.6.cloned.1.call-done = f32[12,128,1]{1,0,2:T(8,128)} async-done(((f32[12,2048,1]{1,0,2:T(8,128)}), f32[12,128,1]{1,0,2:T(8,128)}) %reduce-scatter.6.cloned.1.call-update) | async-done | bytes 6160 | tf_op jit(solution)/shard_map/reduce_scatter | solution.py:55
  252.4 64.7 %reduce-scatter.4.cloned.1.call-done = f32[12,128,1,64]{1,3,0,2:T(8,128)} async-done(((f32[12,2048,1,64]{1,3,0,2:T(8,128)}), f32[12,128,1,64]{1,3,0,2:T(8,128)}) %reduce-scatter.4.cloned.1.call-update) | async-done | bytes 393232 | tf_op jit(solution)/shard_map/reduce_scatter | solution.py:54
  329.9 19.0 %all_gather.10 = f32[2,12,2048,1]{2,1,3,0:T(8,128)S(1)} all-gather(f32[2,12,128,1]{2,1,3,0:T(8,128)S(1)} %pad_maximum_fusion), channel_id=1, replica_groups=mesh['data'=4,'seq'=16] {'seq'}, dimensions={2}, use_global_device_ids=true | all-gather | bytes 208896 | tf_op jit(solution)/shard_map/all_gather | solution.py:84
  350.8 3.7 fusion.77
  354.5 3.7 fusion.76
  358.2 3.7 fusion.36
  362.0 11.9 %all-gather.5.cloned.1.call-done = bf16[12,2048,1,64]{1,3,0,2:T(8,128)(2,1)} async-done(((bf16[12,128,1,64]{1,3,0,2:T(8,128)(2,1)}), bf16[12,2048,1,64]{1,3,0,2:T(8,128)(2,1)}) %all-gather.5.cloned.1.call-update) | async-done | bytes 3145744 | tf_op jit(solution)/shard_map/all_gather | solution.py:83
  373.8 60.8 %multiply_convert_fusion = bf16[12,2048,1024]{1,2,0:T(8,128)(2,1)} fusion(f32[12,2048]{1,0:T(8,128)S(1)} %get-tuple-element.29, bf16[12,2048,1,64]{1,3,0,2:T(8,128)(2,1)} %all-gather.5.cloned.1.call-done, f32[1024,12,64]{0,2,1:T(8,128)} %bitcast.149, f32[12,2048]{1,0:T(8,128)S(1)} %get-tuple-element.28, f32[12,2048]{1,0:T(8,128)S(1)} %bitcast.139, ...), kind=kOutput, calls=%fused_computation | convolution fusion | flops 3423338496 | bytes 157582336 | tf_op jit(solution)/shard_map/kqge,tke->kqgt/dot_general | solution.py:86
  434.6 20.6 %convolution_bitcast_fusion = f32[12,2048,1,64]{1,3,0,2:T(8,128)} fusion(bf16[12,2048,1024]{1,2,0:T(8,128)(2,1)} %multiply_convert_fusion, f32[1024,12,64]{0,2,1:T(8,128)S(1)} %bitcast.127), kind=kOutput, calls=%fused_computation.12 | convolution fusion | flops 3222011904 | bytes 59768832 | tf_op jit(solution)/shard_map/kqgt,tke->kqge/dot_general | solution.py:90
  455.3 9.1 %all-reduce.7.cloned.1.call-start = ((), (), s32[]{:S(2)}) async-start(), calls=%async_computation.9 | async-start | bytes 56623104 | tf_op jit(solution)/shard_map/psum | solution.py:103
  464.4 22.3 %convolution_convert_fusion = bf16[12,64,1024]{2,1,0:T(8,128)(2,1)} fusion(bf16[2048,12,64]{0,2,1:T(8,128)(2,1)S(1)} %copy-done.5, bf16[12,2048,1024]{1,2,0:T(8,128)(2,1)} %multiply_convert_fusion), kind=kOutput, calls=%fused_computation.19 | convolution fusion | flops 3222011904 | bytes 55050240 | tf_op jit(solution)/shard_map/kqgt,qkge->tke/dot_general | solution.py:89
  486.7 4.8 convolution_bitcast_fusion.2
  491.5 38.4 %fusion.12 = bf16[12,64,1024]{2,1,0:T(8,128)(2,1)} fusion(bf16[12,2048,1,64]{1,3,0,2:T(8,128)(2,1)S(1)} %copy-done.37, f32[12,2048,1024]{1,2,0:T(8,128)} %get-tuple-element.33, f32[12,2048]{1,0:T(8,128)S(1)} %get-tuple-element.28, f32[12,2048]{1,0:T(8,128)S(1)} %bitcast.140, pred[1024]{0:T(1024)(128)(4,1)S(1)} %add_compare_fusion), kind=kOutput, calls=%fused_computation.16 | convolution fusion | flops 3347841024 | bytes 105579520 | tf_op jit(solution)/shard_map/kqgt,kqge->tke/dot_general | solution.py:88
  529.9 4.7 convolution_bitcast_fusion.1
  542.0 3.2 bitcast_add_fusion
  545.7 24.8 %all-reduce = (f32[768]{0:T(1024)}, f32[768]{0:T(1024)}) all-reduce(f32[768]{0:T(1024)S(1)} %get-tuple-element.13, f32[768]{0:T(1024)S(1)} %copy-done.31), channel_id=1, replica_groups=mesh['data'=4,'seq'=16] {'seq'}, use_global_device_ids=true, to_apply=%region_12.13 | all-reduce | flops 1536 | bytes 12288 | tf_op jit(solution)/shard_map/psum | solution.py:103
  571.5 274.5 %all-reduce.7.cloned.1.call-done = (f32[768,12,64]{0,2,1:T(8,128)}, f32[768,12,64]{0,2,1:T(8,128)}, f32[768,12,64]{0,2,1:T(8,128)}, f32[12,64,768]{2,1,0:T(8,128...) async-done(((f32[768,12,64]{0,2,1:T(8,128)}, f32[768,12,64]{0,2,1:T(8,128)}, f32[768,12,64]{0,2,1:T(8,128)}, f32[12,64,768]{2,1,0:T(8,128)}, ...) | async-done | bytes 28311568 | tf_op jit(solution)/shard_map/psum | solution.py:103
  845.9 3.4 copy.43
  (150 shorter events, 52.5 us)
Async XLA Ops:
  7.2 315.2 %copy-start = (bf16[2048,768]{1,0:T(8,128)(2,1)S(1)}, bf16[2048,768]{1,0:T(8,128)(2,1)}, u32[]{:S(2)}) copy-start(bf16[2048,768]{1,0:T(8,128)(2,1)} %param.25) | copy-start | bytes 9437188
  7.2 51.6 %all-gather.3.cloned.1.call-start = ((), (), s32[]{:S(2)}) async-start(), calls=%async_computation.3 | async-start | bytes 3342336 | tf_op jit(solution)/shard_map/all_gather | solution.py:39
  12.5 185.5 %all-reduce.5.cloned.1.call-start = ((), (), s32[]{:S(2)}) async-start(), calls=%async_computation.4 | async-start | bytes 262144 | tf_op jit(solution)/shard_map/pmax | solution.py:52
  13.2 5.0 copy-start.38
  13.3 5.0 copy-start.40
  96.0 156.4 %reduce-scatter.6.cloned.1.call-start = ((), (), s32[]{:S(2)}) async-start(), calls=%async_computation.6 | async-start | bytes 139264 | tf_op jit(solution)/shard_map/reduce_scatter | solution.py:55
  96.1 102.0 %copy-start.18 = (f32[12,2048]{1,0:T(8,128)S(1)}, f32[12,2048]{1,0:T(8,128)}, u32[]{:S(2)}) copy-start(f32[12,2048]{1,0:T(8,128)} %get-tuple-element.32) | copy-start | bytes 294916
  199.7 117.5 %reduce-scatter.4.cloned.1.call-start = ((), (), s32[]{:S(2)}) async-start(), calls=%async_computation.5 | async-start | bytes 6684672 | tf_op jit(solution)/shard_map/reduce_scatter | solution.py:54
  236.7 80.4 %copy-start.10 = (bf16[128,768]{1,0:T(8,128)(2,1)S(1)}, bf16[128,768]{1,0:T(8,128)(2,1)}, u32[]{:S(2)}) copy-start(bf16[128,768]{1,0:T(8,128)(2,1)} %param.13) | copy-start | bytes 589828
  236.8 137.0 %all-gather.5.cloned.1.call-start = ((), (), s32[]{:S(2)}) async-start(), calls=%async_computation.7 | async-start | bytes 3342336 | tf_op jit(solution)/shard_map/all_gather | solution.py:83
  328.6 22.2 %copy-start.13 = (f32[128,768]{1,0:T(8,128)}, f32[128,768]{1,0:T(8,128)S(1)}, u32[]{:S(2)}) copy-start(f32[128,768]{1,0:T(8,128)S(1)} %fusion.41) | copy-start | bytes 1179652
  328.6 22.2 %copy-start.22 = (bf16[128,2048]{1,0:T(8,128)(2,1)S(1)}, bf16[128,2048]{1,0:T(8,128)(2,1)}, u32[]{:S(2)}) copy-start(bf16[128,2048]{1,0:T(8,128)(2,1)} %copy-done.21) | copy-start | bytes 1572868
  329.8 204.8 %reduce-scatter.8.cloned.1.call-start = ((), (), s32[]{:S(2)}) async-start(), calls=%async_computation.8 | async-start | bytes 6684672 | tf_op jit(solution)/shard_map/reduce_scatter | solution.py:91
  358.2 15.6 %copy-start.27 = (f32[12,2048,1]{1,0,2:T(8,128)S(1)}, f32[12,2048,1]{1,0,2:T(8,128)}, u32[]{:S(2)}) copy-start(f32[12,2048,1]{1,0,2:T(8,128)} %all-reduce.5.cloned.1.call-done) | copy-start | bytes 294916
  373.8 60.8 %copy-start.2 = (f32[1024,768]{0,1:S(1)}, f32[1024,768]{0,1}, u32[]{:S(2)}) copy-start(f32[1024,768]{0,1} %fusion.71) | copy-start | bytes 9437188
  455.3 9.1 %copy-start.5 = (bf16[2048,12,64]{0,2,1:T(8,128)(2,1)S(1)}, bf16[2048,12,64]{0,2,1:T(8,128)(2,1)}, u32[]{:S(2)}) copy-start(bf16[2048,12,64]{0,2,1:T(8,128)(2,1)} %all-gather.3.cloned.1.call-done) | copy-start | bytes 9437188
  455.3 390.6 %all-reduce.7.cloned.1.call-start = ((), (), s32[]{:S(2)}) async-start(), calls=%async_computation.9 | async-start | bytes 56623104 | tf_op jit(solution)/shard_map/psum | solution.py:103
  529.9 5.8 copy-start.11
  529.9 5.8 copy-start.29
  529.9 5.8 copy-start.33
  541.9 28.6 %copy-start.36 = (f32[128]{0:T(128)S(1)}, f32[128]{0:T(128)}, u32[]{:S(2)}) copy-start(f32[128]{0:T(128)} %copy-done.35) | copy-start | bytes 1540
  542.0 28.6 %copy-start.14 = (f32[128,768]{1,0:T(8,128)S(1)}, f32[128,768]{1,0:T(8,128)}, u32[]{:S(2)}) copy-start(f32[128,768]{1,0:T(8,128)} %copy-done.13) | copy-start | bytes 1179652
  849.3 6.0 slice-start.4
  855.3 7.5 slice-start
  (32 other events, 98.3 us)
Sparse Core Ops, SparseCore 0:
  12.6 46.1 all-gather.2
  96.1 101.8 all-reduce.4
  200.9 51.4 reduce-scatter.5
  255.2 61.8 reduce-scatter.3
  329.9 43.8 all-gather.4
  455.5 59.1 reduce-scatter.7
  537.8 308.0 all-reduce.6
where the time goes:
time: 879 us; the launch traced here: 875 us
  waiting for transfers between devices  474 us (54%)
  matrix products  268 us (30%)
  blocking collectives  43.9 us (5%)
  other arithmetic  37.8 us (4%)
  local copies, waits for them, and re-layouts  25.8 us (3%)
  between operations  15.4 us (2%)
  starting transfers between devices  9.69 us (1%)
    psum x1, waiting for transfers between devices, device_step(): lax.psum((g_norm_attn, g_wq, g_wk, g_wv, g_wo, g_norm_mlp, g_gate, g_up,...  274 us
    pmax x1, waiting for transfers between devices, device_step(): global_max = lax.pmax(local_max, 'seq')  70.6 us
    reduce_scatter x1, waiting for transfers between devices, device_step(): lax.psum_scatter(local_out * rescale[..., None], 'seq', scatter_dimension...  64.7 us
    dot_general x1, matrix products, device_step(): jnp.einsum('kqge,tke->kqgt', grad_att_all, mem_vals, preferred_element_ty...  60.8 us
    dot_general x1, matrix products, device_step(): jnp.einsum('kqgt,kqge->tke', attn_prob.astype(jnp.bfloat16), grad_att_all...  38.4 us
    all_gather x1, waiting for transfers between devices, device_step(): lax.all_gather(local_query, 'seq', axis=0, tiled=True)  37.5 us
    dot_general x1, matrix products, masked_scores(): jnp.einsum('qkge,tke->kqgt', dec_query, mem_keys, preferred_element_type=...  37.1 us
    dot_general x1, matrix products, device_step(): jnp.einsum('kqgt,tke->kqge', exp_scores.astype(jnp.bfloat16), mem_vals, p...  37 us
  transfers between devices with their start and end apart: 7, of which 6 were waited for; matrix products, arithmetic and copies ran while one was open for 19% of the time, Pallas kernels for 0%

commit v1 on v0

v1 whole, which is shorter than its diff:
```python
import functools
import math

import jax
import jax.numpy as jnp
from jax import lax
from jax.experimental import pallas as pl
from jax.experimental.pallas import tpu as pltpu
from jax.sharding import PartitionSpec as P

F32 = jnp.float32
BF16 = jnp.bfloat16
QT = 256
MC = 256
LOG2E = math.log2(math.e)
VMEM = pltpu.VMEM


def mm(a, b):
    return jnp.dot(a, b, preferred_element_type=F32)


def mm_bt(a, b):
    return lax.dot_general(a, b, (((1,), (1,)), ((), ())), preferred_element_type=F32)


def mm_at(a, b):
    return lax.dot_general(a, b, (((0,), (0,)), ((), ())), preferred_element_type=F32)


def rms_norm(tensor, gain):
    mean_sq = jnp.mean(tensor * tensor, axis=-1, keepdims=True)
    return tensor * lax.rsqrt(mean_sq + 1e-6) * gain


def gated_unit(gate_pre, up_pre):
    return jax.nn.silu(gate_pre) * up_pre


def split3(x):
    hi = lax.reduce_precision(x, 8, 7)
    rest = x - hi
    mid = lax.reduce_precision(rest, 8, 7)
    lo = rest - mid
    return hi.astype(BF16), mid.astype(BF16), lo.astype(BF16)


def fwd_kernel(heads, mem, queries, c, k_ref, ak_ref, vt_ref, qz_ref, aq_ref, o_ref, m_ref, l_ref, s_scr, mx_scr):
    nq = queries // QT
    n = heads * nq

    def step(ia, sa, ib, sb):
        if ia is not None:
            h = ia // nq
            qc = ia - h * nq
            rhs = jnp.concatenate([qz_ref[pl.ds(pl.multiple_of(h * 128, 128), 128), pl.ds(pl.multiple_of(qc * QT, QT), QT)], aq_ref[...]], axis=0)
            pair = pl.ds(pl.multiple_of((h // 2) * 128, 128), 128)
            mx = None
        if ib is not None:
            hb = ib // nq
            qb = ib - hb * nq
            m = jnp.max(mx_scr[sb], axis=0, keepdims=True)
            vrow = pl.ds(pl.multiple_of(hb * 64, 64), 64)
            ls = None
            acc = None
        for j in range(mem // MC):
            rows = slice(j * MC, (j + 1) * MC)
            if ia is not None:
                s = mm(jnp.concatenate([k_ref[rows, pair], ak_ref[rows, 0:16]], axis=1), rhs)
                s_scr[sa, rows, :] = s
                t = jnp.max(s.reshape(MC // 8, 8, QT), axis=0)
                mx = t if mx is None else jnp.maximum(mx, t)
            if ib is not None:
                pr = jnp.exp2((s_scr[sb, rows, :] - m) * c)
                t = jnp.sum(pr.reshape(MC // 8, 8, QT), axis=0)
                ls = t if ls is None else ls + t
                d = mm(vt_ref[vrow, rows], pr.astype(BF16))
                acc = d if acc is None else acc + d
        if ia is not None:
            mx_scr[sa] = mx
        if ib is not None:
            qs = pl.ds(pl.multiple_of(qb * QT, QT), QT)
            o_ref[vrow, qs] = acc
            m_ref[pl.ds(hb, 1), qs] = m
            l_ref[pl.ds(hb, 1), qs] = jnp.sum(ls, axis=0, keepdims=True)

    step(0, 0, None, None)

    def body(i, carry):
        step(2 * i + 1, 1, 2 * i, 0)
        step(jnp.minimum(2 * i + 2, n - 1), 0, 2 * i + 1, 1)
        return carry

    lax.fori_loop(0, n // 2, body, 0)


def bwd_kernel(heads, mem, queries, c, k_ref, v_ref, ak_ref, kt_ref, qz_ref, aq_ref, doz_ref, ad_ref, dkt_ref, dvt_ref, dqt_ref):
    nq = queries // QT
    nm = mem // MC
    dkt_ref[...] = jnp.zeros_like(dkt_ref)
    dvt_ref[...] = jnp.zeros_like(dvt_ref)

    def body(it, carry):
        h = it // nq
        qc = it - h * nq
        pair = h // 2
        qs = pl.ds(pl.multiple_of(qc * QT, QT), QT)
        hz = pl.ds(pl.multiple_of(h * 128, 128), 128)
        h64 = pl.ds(pl.multiple_of(h * 64, 64), 64)
        h16 = pl.ds(pl.multiple_of(h * 16, 16), 16)
        ps = pl.ds(pl.multiple_of(pair * 128, 128), 128)
        hz64 = pl.ds(pl.multiple_of(h * 128 + (h - 2 * pair) * 64, 64), 64)
        q_t = qz_ref[hz64, qs]
        do_t = doz_ref[hz64, qs]
        r1 = jnp.concatenate([qz_ref[hz, qs], aq_ref[h16, qs]], axis=0)
        r2 = jnp.concatenate([doz_ref[hz, qs], ad_ref[h16, qs]], axis=0)
        stage = {}
        dq = None
        for j in range(nm + 2):
            if j < nm:
                rows = slice(j * MC, (j + 1) * MC)
                ak = ak_ref[rows, 0:16]
                stage["a", j] = (mm(jnp.concatenate([k_ref[rows, ps], ak], axis=1), r1),
                                 mm(jnp.concatenate([v_ref[rows, ps], ak], axis=1), r2))
            if 1 <= j <= nm:
                s, dp = stage.pop(("a", j - 1))
                a = jnp.exp2(s * c)
                stage["b", j - 1] = (a.astype(BF16), (a * dp).astype(BF16))
            if j >= 2:
                rows = slice((j - 2) * MC, (j - 1) * MC)
                pb, ds = stage.pop(("b", j - 2))
                dvt_ref[h64, rows] += mm_bt(do_t, pb)
                dkt_ref[h64, rows] += mm_bt(q_t, ds)
                d = mm(kt_ref[h64, rows], ds)
                dq = d if dq is None else dq + d
        dqt_ref[h64, qs] = dq
        return carry

    lax.fori_loop(0, heads * nq, body, 0)


def vspec(n):
    return [pl.BlockSpec(memory_space=VMEM)] * n


def params():
    return pltpu.CompilerParams(vmem_limit_bytes=60 * 1024 * 1024)


def solution(mesh):
    group = mesh.shape['seq']
    row_spec = P(('data', 'seq'), None)
    part_vec = P('data')
    part_mat = P('data', None)
    part_cube = P('data', None, None)

    def device_step(dec_in, memory, mem_len, grad_out, norm_attn, wq, wk, wv, wo, norm_mlp, w_gate, w_up, w_down):
        rows, dim = dec_in.shape
        mem = memory.shape[0]
        heads, hd = wq.shape[1], wq.shape[2]
        inner = heads * hd
        queries = rows * group
        c = LOG2E * hd ** -0.5
        wq2, wk2, wv2 = (w.reshape(dim, inner) for w in (wq, wk, wv))
        wo2 = wo.reshape(inner, dim)
        gain1 = norm_attn.astype(F32)
        gain2 = norm_mlp.astype(F32)

        y_all = lax.all_gather(dec_in, 'seq', axis=0, tiled=True)
        go_all = lax.all_gather(grad_out.astype(BF16), 'seq', axis=0, tiled=True)
        x_all = y_all.astype(F32)
        n1_all = rms_norm(x_all, gain1).astype(BF16)
        q_t = lax.dot_general(wq2, n1_all, (((0,), (1,)), ((), ())), preferred_element_type=F32).astype(BF16)

        def pair_pad(t):
            t = t.reshape(heads // 2, 2, hd, queries)
            zero = jnp.zeros_like(t[:, 0])
            return jnp.stack([t[:, 0], zero, zero, t[:, 1]], axis=1).reshape(heads * 128, queries)

        qz = pair_pad(q_t)
        mem_k = mm(memory, wk2).astype(BF16)
        mem_v = mm(memory, wv2).astype(BF16)
        k_t = mem_k.T
        v_t = mem_v.T
        pos = lax.axis_index('seq') * mem + jnp.arange(mem)
        bias = jnp.where(pos < mem_len[0], 0.0, -1e30).astype(F32)
        lane = jnp.arange(128)
        ak = jnp.where(lane[None, :] == 0, bias[:, None], jnp.where(lane[None, :] < 4, 1.0, 0.0)).astype(BF16)
        aq0 = jnp.where(jnp.arange(16)[:, None] == 0, 1.0, 0.0).astype(BF16) * jnp.ones((1, QT), BF16)

        o_t, m_loc, l_loc = pl.pallas_call(
            functools.partial(fwd_kernel, heads, mem, queries, c),
            out_shape=(jax.ShapeDtypeStruct((inner, queries), F32), jax.ShapeDtypeStruct((heads, queries), F32), jax.ShapeDtypeStruct((heads, queries), F32)),
            in_specs=vspec(5), out_specs=tuple(vspec(3)),
            scratch_shapes=[VMEM((2, mem, QT), F32), VMEM((2, 8, QT), F32)],
            compiler_params=params(),
            cost_estimate=pl.CostEstimate(flops=4 * heads * mem * queries * 256, bytes_accessed=30 << 20, transcendentals=0),
            name="attn_fwd")(mem_k, ak, v_t, qz, aq0)
        m_all = lax.pmax(m_loc, 'seq')
        scale_loc = jnp.exp2((m_loc - m_all) * c)
        o_part = (o_t.reshape(heads, hd, queries) * scale_loc[:, None, :]).reshape(inner, queries).T
        l_part = (l_loc * scale_loc).T
        packed = jnp.concatenate([o_part, l_part, jnp.zeros((queries, 128 - heads), F32)], axis=1)
        summed = lax.psum_scatter(packed, 'seq', scatter_dimension=0, tiled=True)
        den = summed[:, inner:inner + heads]
        attended_f = (summed[:, :inner].reshape(rows, heads, hd) / den[:, :, None]).reshape(rows, inner)
        attended = attended_f.astype(BF16)
        m_own = lax.dynamic_slice_in_dim(m_all, lax.axis_index('seq') * rows, rows, axis=1).T
        lse = m_own + jnp.log2(den) / c

        x_in = dec_in.astype(F32)
        hidden = (x_in + mm(attended, wo2)).astype(BF16)
        n2_f, n2_pull = jax.vjp(rms_norm, hidden.astype(F32), gain2)
        n2 = n2_f.astype(BF16)
        gate_pre = mm(n2, w_gate)
        up_pre = mm(n2, w_up)
        _, gated_pull = jax.vjp(gated_unit, gate_pre, up_pre)
        grad_act = mm_bt(grad_out.astype(BF16), w_down)
        grad_gate, grad_up = gated_pull(grad_act)
        grad_n2 = mm_bt(grad_gate.astype(BF16), w_gate) + mm_bt(grad_up.astype(BF16), w_up)
        grad_h_norm, g_norm_mlp_part = n2_pull(grad_n2)
        grad_hidden = grad_out + grad_h_norm
        dh = grad_hidden.astype(BF16)
        d_att = mm_bt(dh, wo2)
        delta = jnp.sum((d_att * attended_f).reshape(rows, heads, hd), axis=-1)

        stats = jnp.concatenate(split3(-lse) + split3(-delta) + (jnp.zeros((rows, 128 - 6 * heads), BF16),), axis=1)
        gn = jnp.stack(split3(g_norm_mlp_part) + (jnp.zeros((dim,), BF16),) * 13)
        payload = jnp.concatenate([jnp.concatenate([dh, stats], axis=1), jnp.concatenate([gn, jnp.zeros((16, 128), BF16)], axis=1)], axis=0)
        gathered = lax.all_gather(payload, 'seq', axis=0, tiled=False)
        dh_all = gathered[:, :rows, :dim].reshape(queries, dim)
        st = gathered[:, :rows, dim:dim + 6 * heads].reshape(queries, 6, heads).transpose(2, 1, 0)
        g_norm_mlp = jnp.sum(gathered[:, rows:rows + 3, :dim].astype(F32), axis=(0, 1))
        one = jnp.ones((heads, 1, queries), BF16)
        pad = jnp.zeros((heads, 12, queries), BF16)
        aq = jnp.concatenate([one, st[:, 0:3], pad], axis=1).reshape(heads * 16, queries)
        ad = jnp.concatenate([0 * one, st[:, 3:6], pad], axis=1).reshape(heads * 16, queries)
        doz = pair_pad(mm_bt(wo2, dh_all).astype(BF16))

        dk_t, dv_t, dq_t = pl.pallas_call(
            functools.partial(bwd_kernel, heads, mem, queries, c),
            out_shape=(jax.ShapeDtypeStruct((inner, mem), F32), jax.ShapeDtypeStruct((inner, mem), F32), jax.ShapeDtypeStruct((inner, queries), F32)),
            in_specs=vspec(8), out_specs=tuple(vspec(3)),
            compiler_params=params(),
            cost_estimate=pl.CostEstimate(flops=10 * heads * mem * queries * 256, bytes_accessed=40 << 20, transcendentals=0),
            name="attn_bwd")(mem_k, mem_v, ak, k_t, qz, aq, doz, ad)
        att_all = lax.all_gather(attended, 'seq', axis=0, tiled=True)
        score_scale = hd ** -0.5
        dq = lax.psum_scatter(dq_t.T, 'seq', scatter_dimension=0, tiled=True) * score_scale
        dq_b = dq.astype(BF16)
        dq_all = lax.all_gather(dq_b, 'seq', axis=0, tiled=True)
        dkb = (dk_t * score_scale).astype(BF16)
        dvb = dv_t.astype(BF16)
        dkv = jnp.concatenate([dkb, dvb], axis=0)
        g_wkv = lax.psum(lax.dot_general(dkv, memory, (((1,), (0,)), ((), ())), preferred_element_type=F32), 'seq').T
        g_mem = lax.dot_general(dkv, jnp.concatenate([wk2, wv2], axis=1), (((0,), (1,)), ((), ())), preferred_element_type=F32)

        _, norm_pull = jax.vjp(rms_norm, x_in, gain1)
        grad_x_norm, _ = norm_pull(mm_bt(dq_b, wq2))
        g_dec = grad_hidden + grad_x_norm

        xhat = x_all * lax.rsqrt(jnp.mean(x_all * x_all, axis=-1, keepdims=True) + 1e-6)
        g_norm_attn = jnp.sum(mm_bt(dq_all, wq2) * xhat, axis=0)
        g_wq = mm_at(n1_all, dq_all)
        g_wo = mm_at(att_all, dh_all)
        h_all = (x_all + mm(att_all, wo2)).astype(BF16)
        n2_all = rms_norm(h_all.astype(F32), gain2).astype(BF16)
        mlp_f, pull_all = jax.vjp(gated_unit, mm(n2_all, w_gate), mm(n2_all, w_up))
        gg, gu = pull_all(mm_bt(go_all, w_down))
        g_down = mm_at(mlp_f.astype(BF16), go_all)
        g_gate = mm_at(n2_all, gg.astype(BF16))
        g_up = mm_at(n2_all, gu.astype(BF16))
        cube = (dim, heads, hd)
        return (g_dec, g_mem, g_norm_attn, g_wq.reshape(cube), g_wkv[:, :inner].reshape(cube), g_wkv[:, inner:].reshape(cube),
                g_wo.reshape(heads, hd, dim), g_norm_mlp, g_gate, g_up, g_down)

    return jax.shard_map(device_step, mesh=mesh,
                         in_specs=(row_spec, row_spec, part_vec, row_spec) + (P(),) * 9,
                         out_specs=(row_spec, row_spec, part_vec, part_cube, part_cube, part_cube, part_cube, part_vec, part_mat, part_mat, part_mat),
                         check_vma=False)
```

time: 879 us -> 693 us (0.79)
  waiting for transfers between devices: 474 us -> 331 us
  Pallas kernels: 0 us -> 121 us
  matrix products: 268 us -> 157 us
  blocking collectives: 43.9 us -> 0 us
    psum x1, waiting for transfers between devices: 274 us -> 64.5 us  [device_step(): lax.psum(lax.dot_general(dkv, memory, (((1,), (0,)), ((), ())), preferred...]
    pallas_call x0 -> x2, Pallas kernels: none -> 121 us  [the longest x1 79.9 us: device_step(): pl.pallas_call(functools.partial(bwd_kernel, heads, mem, queries, c), out...]
    dot_general x22 -> x23, matrix products: 256 us -> 157 us  [the longest x5 64 us: mm_at(): lax.dot_general(a, b, (((0,), (0,)), ((), ())), preferred_element_type=F32)]
    all_gather x2 -> x5, waiting for transfers between devices: 49.4 us -> 105 us  [the longest x1 39.3 us: device_step(): gathered = lax.all_gather(payload, 'seq', axis=0, tiled=False)]
    pmax x1, waiting for transfers between devices: 70.6 us -> 101 us  [device_step(): m_all = lax.pmax(m_loc, 'seq')]
    reduce_sum x1 -> x2, other arithmetic: 31.4 us -> 1.61 us  [the longest x1 1.57 us: device_step(): jnp.sum(gathered[:, rows:rows + 3, :dim].astype(F32), axis=(0, 1))]
    psum x1 -> x0, blocking collectives: 24.8 us -> none  [device_step(): lax.psum((g_norm_attn, g_wq, g_wk, g_wv, g_wo, g_norm_mlp, g_gate, g_up,...]
    reduce_scatter x3 -> x2, waiting for transfers between devices: 79.7 us -> 57.6 us  [the longest x1 57.6 us: device_step(): summed = lax.psum_scatter(packed, 'seq', scatter_dimension=0, tiled=True)]
  transfers between devices with their start and end apart: 7 -> 9, of which waited for: 6 -> 6; matrix products, arithmetic and copies ran while one was open for 19% -> 23% of each run, Pallas kernels for 0% -> 12%
where the time goes in v1:
time: 693 us; the launch traced here: 686 us
  waiting for transfers between devices  331 us (48%)
  matrix products  157 us (23%)
  Pallas kernels  121 us (17%)
  other arithmetic  31.1 us (4%)
  local copies, waits for them, and re-layouts  30.3 us (4%)
  between operations  15.6 us (2%)
    pmax x1, waiting for transfers between devices, device_step(): m_all = lax.pmax(m_loc, 'seq')  101 us
    pallas_call x1, Pallas kernels, device_step(): pl.pallas_call(functools.partial(bwd_kernel, heads, mem, queries, c), out...  79.9 us
    psum x1, waiting for transfers between devices, device_step(): lax.psum(lax.dot_general(dkv, memory, (((1,), (0,)), ((), ())), preferred...  64.5 us
    dot_general x5, matrix products, mm_at(): lax.dot_general(a, b, (((0,), (0,)), ((), ())), preferred_element_type=F32)  64 us
    reduce_scatter x1, waiting for transfers between devices, device_step(): summed = lax.psum_scatter(packed, 'seq', scatter_dimension=0, tiled=True)  57.6 us
    pallas_call x1, Pallas kernels, device_step(): pl.pallas_call(functools.partial(fwd_kernel, heads, mem, queries, c), out...  41.1 us
    all_gather x1, waiting for transfers between devices, device_step(): gathered = lax.all_gather(payload, 'seq', axis=0, tiled=False)  39.3 us
    dot_general x7, matrix products, mm(): return jnp.dot(a, b, preferred_element_type=F32)  38.2 us
  transfers between devices with their start and end apart: 9, of which 6 were waited for; matrix products, arithmetic and copies ran while one was open for 23% of the time, Pallas kernels for 12%

profile of v1, /device:TPU:21, one launch (start us, length us, event | category | flops | bytes accessed | tf_op | source)
XLA Modules:
  0.0 686.3 jit_solution(4942437509977483096)
XLA Ops:
  9.5 4.3 convolution_convert_fusion.3
  16.4 4.3 convolution_convert_fusion.2.v_ref
  24.3 28.0 %all-gather.7.cloned.1.call-done = bf16[2048,768]{1,0:T(8,128)(2,1)} async-done(((bf16[128,768]{1,0:T(8,128)(2,1)}), bf16[2048,768]{1,0:T(8,128)(2,1)}) %all-gather.7.cloned.1.call-update) | async-done | bytes 3145744 | tf_op jit(solution)/shard_map/all_gather | solution.py:169
  55.1 4.3 convolution_convert_fusion.1
  63.5 41.1 %attn_fwd.1 = (f32[768,2048]{1,0:T(8,128)}, f32[12,2048]{1,0:T(8,128)}, f32[12,2048]{1,0:T(8,128)}) custom-call(bf16[1024,768]{1,0:T(8,128)(2,1)} %copy.59.k_ref, bf16[1024,128]{1,0:T(8,128)(2,1)} %select_convert_fusion.ak_ref, bf16[768,1024]{1,0:T(8,128)(2,1)} %copy.60.vt_ref, bf16[1536,2048]{1,0:T(8,128)(2,1)} %bitcast.83, bf16[16,256]{1,0:T(8,128)(2,1)} %mul.243.aq_ref), custom_call_target="tpu_custom_call" | custom-call | flops 25769803776 | bytes 31457280 | tf_op jit(solution)/shard_map/attn_fwd/pallas_call | solution.py:191
  104.8 100.9 %all-reduce.4.cloned.1.call-done = f32[12,2048]{1,0:T(8,128)} async-done(((f32[12,2048]{1,0:T(8,128)}), f32[12,2048]{1,0:T(8,128)}) %all-reduce.4.cloned.1.call-update) | async-done | bytes 98320 | tf_op jit(solution)/shard_map/pmax | solution.py:199
  220.0 57.6 %reduce-scatter.3.cloned.1.call-done = f32[128,896]{0,1:T(8,128)} async-done(((f32[2048,896]{0,1:T(8,128)}), f32[128,896]{0,1:T(8,128)}) %reduce-scatter.3.cloned.1.call-update) | async-done | bytes 458768 | tf_op jit(solution)/shard_map/reduce_scatter | solution.py:204
  285.9 5.1 fusion.28
  300.3 39.3 %all-gather.15.cloned.1.call-done = bf16[2304,896]{1,0:T(8,128)(2,1)} async-done(((bf16[144,896]{1,0:T(8,128)(2,1)}), bf16[2304,896]{1,0:T(8,128)(2,1)}) %all-gather.15.cloned.1.call-update) | async-done | bytes 4128784 | tf_op jit(solution)/shard_map/all_gather | solution.py:230
  349.0 4.8 convolution_convert_fusion
  359.3 79.9 %attn_bwd.1 = (f32[768,1024]{1,0:T(8,128)}, f32[768,1024]{1,0:T(8,128)}, f32[768,2048]{1,0:T(8,128)}) custom-call(bf16[1024,768]{1,0:T(8,128)(2,1)} %copy.59.k_ref, bf16[1024,768]{1,0:T(8,128)(2,1)} %convolution_convert_fusion.2.v_ref, bf16[1024,128]{1,0:T(8,128)(2,1)} %select_convert_fusion.ak_ref, bf16[768,1024]{1,0:T(8,128)(2,1)} %bitcast.100, ...), custom_call_target="tpu_custom_call" | custom-call | flops 64424509440 | bytes 41943040 | tf_op jit(solution)/shard_map/attn_bwd/pallas_call | solution.py:240
  439.6 12.7 %fusion.72 = f32[2048,2048]{1,0:T(8,128)} fusion(bf16[2048,768]{1,0:T(8,128)(2,1)} %all-gather.13.cloned.1.call-done, bf16[2048,768]{1,0:T(8,128)(2,1)} %param.25), kind=kOutput, calls=%fused_computation.130 | convolution fusion | flops 6442450944 | bytes 23068672 | tf_op jit(solution)/shard_map/dot_general | solution.py:24
  452.3 6.3 fusion.12
  458.6 9.9 %fusion.58 = f32[2048,2048]{1,0:T(8,128)} fusion(bf16[768,2048]{1,0:T(8,128)(2,1)S(1)} %copy-done, bf16[2048,768]{1,0:T(8,128)(2,1)S(1)} %get-tuple-element.61, f32[768]{0:T(1024)S(1)} %convert_element_type.166, f32[2048]{0:T(1024)S(1)} %add_rsqrt_fusion), kind=kOutput, calls=%fused_computation.120 | convolution fusion | flops 6448742400 | bytes 23079936 | tf_op jit(solution)/shard_map/dot_general | solution.py:20
  468.5 10.0 %fusion.60 = f32[2048,2048]{1,0:T(8,128)} fusion(bf16[768,2048]{1,0:T(8,128)(2,1)S(1)} %copy-done.26, bf16[2048,768]{1,0:T(8,128)(2,1)S(1)} %get-tuple-element.61, f32[768]{0:T(1024)S(1)} %convert_element_type.166, f32[2048]{0:T(1024)S(1)} %add_rsqrt_fusion), kind=kOutput, calls=%fused_computation.121 | convolution fusion | flops 6448742400 | bytes 23079936 | tf_op jit(solution)/shard_map/dot_general | solution.py:20
  478.5 22.0 %fusion.6 = f32[768,2048]{1,0:T(8,128)} fusion(f32[2048,2048]{1,0:T(8,128)} %fusion.58, f32[2048,2048]{1,0:T(8,128)} %fusion.72, f32[2048,2048]{1,0:T(8,128)} %fusion.60, bf16[2048,768]{1,0:T(8,128)(2,1)S(1)} %get-tuple-element.61, f32[768]{0:T(1024)S(1)} %convert_element_type.166, f32[2048]{0:T(1024)S(1)} %add_rsqrt_fusion), kind=kOutput, calls=%fused_computation.13 | convolution fusion | flops 6494879744 | bytes 59780096 | tf_op jit(solution)/shard_map/dot_general | solution.py:28
  504.5 5.4 convolution_bitcast_fusion
  511.8 16.5 %fusion.5 = f32[2048,768]{1,0:T(8,128)} fusion(bf16[2048,768]{1,0:T(8,128)(2,1)S(1)} %copy-done.28, f32[2048,2048]{1,0:T(8,128)} %fusion.60, f32[2048,2048]{1,0:T(8,128)} %fusion.58), kind=kOutput, calls=%fused_computation.12 | convolution fusion | flops 6467616768 | bytes 42991616 | tf_op jit(solution)/shard_map/dot_general | solution.py:28
  530.1 17.4 %fusion.4 = f32[768,2048]{1,0:T(8,128)} fusion(f32[2048,2048]{1,0:T(8,128)} %fusion.72, f32[2048,2048]{1,0:T(8,128)} %fusion.58, bf16[2048,768]{1,0:T(8,128)(2,1)} %copy-done.31, f32[768]{0:T(1024)S(1)} %convert_element_type.166, f32[2048]{0:T(1024)S(1)} %add_rsqrt_fusion), kind=kOutput, calls=%fused_computation.11 | convolution fusion | flops 6473908224 | bytes 43002880 | tf_op jit(solution)/shard_map/dot_general | solution.py:28
  549.1 6.6 fusion.19
  559.7 64.5 %all-reduce.6.cloned.1.call-done = f32[768,1536]{0,1:T(8,128)} async-done(((f32[768,1536]{0,1:T(8,128)}), f32[768,1536]{0,1:T(8,128)}) %all-reduce.6.cloned.1.call-update) | async-done | bytes 4718608 | tf_op jit(solution)/shard_map/psum | solution.py:255
  624.2 4.9 fusion.66
  630.5 38.2 %all-gather.9.cloned.1.call-done = bf16[2048,768]{0,1:T(8,128)(2,1)} async-done(((bf16[128,768]{0,1:T(8,128)(2,1)}), bf16[2048,768]{0,1:T(8,128)(2,1)}) %all-gather.9.cloned.1.call-update) | async-done | bytes 3145744 | tf_op jit(solution)/shard_map/all_gather | solution.py:251
  668.7 6.4 fusion.11
  (158 shorter events, 80.3 us)
Async XLA Ops:
  7.2 277.1 %copy-start = (bf16[768,2048]{1,0:T(8,128)(2,1)S(1)}, bf16[768,2048]{1,0:T(8,128)(2,1)}, u32[]{:S(2)}) copy-start(bf16[768,2048]{1,0:T(8,128)(2,1)} %param.23) | copy-start | bytes 9437188
  7.2 45.0 %all-gather.7.cloned.1.call-start = ((), (), s32[]{:S(2)}) async-start(), calls=%async_computation.2 | async-start | bytes 3342336 | tf_op jit(solution)/shard_map/all_gather | solution.py:169
  8.0 197.7 %all-reduce.4.cloned.1.call-start = ((), (), s32[]{:S(2)}) async-start(), calls=%async_computation.3 | async-start | bytes 262144 | tf_op jit(solution)/shard_map/pmax | solution.py:199
  9.5 45.5 %copy-start.19 = (f32[768]{0:T(1024)}, f32[768]{0:T(1024)S(1)}, u32[]{:S(2)}) copy-start(f32[768]{0:T(1024)S(1)} %convert_element_type.158) | copy-start | bytes 9220
  23.3 36.3 %copy-start.23 = (bf16[4]{0:T(256)(128)(2,1)}, bf16[4]{0:T(256)(128)(2,1)S(1)}, u32[]{:S(2)}) copy-start(bf16[4]{0:T(256)(128)(2,1)S(1)} %pad.20.clone) | copy-start | bytes 28
  104.7 173.0 %reduce-scatter.3.cloned.1.call-start = ((), (), s32[]{:S(2)}) async-start(), calls=%async_computation.4 | async-start | bytes 7798784 | tf_op jit(solution)/shard_map/reduce_scatter | solution.py:204
  214.3 125.3 %all-gather.15.cloned.1.call-start = ((), (), s32[]{:S(2)}) async-start(), calls=%async_computation.10 | async-start | bytes 4386816 | tf_op jit(solution)/shard_map/all_gather | solution.py:230
  216.0 66.5 %copy-start.9 = (bf16[128,768]{1,0:T(8,128)(2,1)}, bf16[128,768]{1,0:T(8,128)(2,1)S(1)}, u32[]{:S(2)}) copy-start(bf16[128,768]{1,0:T(8,128)(2,1)S(1)} %convert_element_type.151) | copy-start | bytes 589828
  299.0 140.6 %all-gather.13.cloned.1.call-start = ((), (), s32[]{:S(2)}) async-start(), calls=%async_computation.9 | async-start | bytes 3342336 | tf_op jit(solution)/shard_map/all_gather | solution.py:170
  299.6 152.6 %all-gather.11.cloned.1.call-start = ((), (), s32[]{:S(2)}) async-start(), calls=%async_computation.8 | async-start | bytes 3342336 | tf_op jit(solution)/shard_map/all_gather | solution.py:247
  300.3 228.1 %reduce-scatter.5.cloned.1.call-start = ((), (), s32[]{:S(2)}) async-start(), calls=%async_computation.5 | async-start | bytes 6684672 | tf_op jit(solution)/shard_map/reduce_scatter | solution.py:249
  439.3 184.9 %all-reduce.6.cloned.1.call-start = ((), (), s32[]{:S(2)}) async-start(), calls=%async_computation.7 | async-start | bytes 9437184 | tf_op jit(solution)/shard_map/psum | solution.py:255
  458.5 20.0 %copy-start.31 = (bf16[2048,768]{1,0:T(8,128)(2,1)}, bf16[2048,768]{1,0:T(8,128)(2,1)S(1)}, u32[]{:S(2)}) copy-start(bf16[2048,768]{1,0:T(8,128)(2,1)S(1)} %get-tuple-element.61) | copy-start | bytes 9437188
  458.6 10.0 %copy-start.26 = (bf16[768,2048]{1,0:T(8,128)(2,1)S(1)}, bf16[768,2048]{1,0:T(8,128)(2,1)}, u32[]{:S(2)}) copy-start(bf16[768,2048]{1,0:T(8,128)(2,1)} %param.24) | copy-start | bytes 9437188
  478.5 22.0 %copy-start.8 = (f32[768,1024]{1,0:T(8,128)S(1)}, f32[768,1024]{1,0:T(8,128)}, u32[]{:S(2)}) copy-start(f32[768,1024]{1,0:T(8,128)} %get-tuple-element.22) | copy-start | bytes 9437188
  510.0 158.7 %all-gather.9.cloned.1.call-start = ((), (), s32[]{:S(2)}) async-start(), calls=%async_computation.6 | async-start | bytes 3342336 | tf_op jit(solution)/shard_map/all_gather | solution.py:251
  530.1 19.0 %copy-start.14 = (bf16[768,1024]{1,0:T(8,128)(2,1)S(1)}, bf16[768,1024]{1,0:T(8,128)(2,1)}, u32[]{:S(2)}) copy-start(bf16[768,1024]{1,0:T(8,128)(2,1)} %copy-done.13) | copy-start | bytes 4718596
  549.1 6.7 copy-start.27
  559.7 69.4 %copy-start.3 = (bf16[128,768]{1,0:T(8,128)(2,1)S(1)}, bf16[128,768]{1,0:T(8,128)(2,1)}, u32[]{:S(2)}) copy-start(bf16[128,768]{1,0:T(8,128)(2,1)} %param.13) | copy-start | bytes 589828
  559.7 69.4 %copy-start.10 = (bf16[128,768]{0,1:T(8,128)(2,1)S(1)}, bf16[128,768]{0,1:T(8,128)(2,1)}, u32[]{:S(2)}) copy-start(bf16[128,768]{0,1:T(8,128)(2,1)} %multiply_convert_fusion.7) | copy-start | bytes 589828
  559.7 69.4 %copy-start.18 = (bf16[768,12,64]{0,2,1:T(8,128)(2,1)S(1)}, bf16[768,12,64]{0,2,1:T(8,128)(2,1)}, u32[]{:S(2)}) copy-start(bf16[768,12,64]{0,2,1:T(8,128)(2,1)} %param.18) | copy-start | bytes 3538948
  559.7 69.4 %copy-start.20 = (f32[768]{0:T(1024)S(1)}, f32[768]{0:T(1024)}, u32[]{:S(2)}) copy-start(f32[768]{0:T(1024)} %copy-done.19) | copy-start | bytes 9220
  559.7 69.9 %copy-start.16 = (f32[128,768]{1,0:T(8,128)S(1)}, f32[128,768]{1,0:T(8,128)}, u32[]{:S(2)}) copy-start(f32[128,768]{1,0:T(8,128)} %get-tuple-element.30) | copy-start | bytes 1179652
  629.1 39.6 %copy-start.22 = (f32[2048]{0:T(1024)S(1)}, f32[2048]{0:T(1024)}, u32[]{:S(2)}) copy-start(f32[2048]{0:T(1024)} %copy-done.21) | copy-start | bytes 24580
  (17 other events, 58.6 us)
Sparse Core Ops, SparseCore 0:
  9.7 42.5 all-gather.6
  104.8 100.9 all-reduce.3
  214.4 63.1 reduce-scatter.2
  299.1 40.5 all-gather.14
  341.1 35.9 all-gather.12
  378.6 39.4 all-gather.10
  439.4 58.6 reduce-scatter.4
  510.1 114.0 all-reduce.5
  626.4 42.2 all-gather.8

commit v2 on v1

--- a/solution.py
+++ b/solution.py
@@ -14,6 +14,7 @@
 MC = 256
 LOG2E = math.log2(math.e)
 VMEM = pltpu.VMEM
+MESH = pl.DeviceIdType.MESH
 
 
 def mm(a, b):
@@ -45,53 +46,285 @@
     return hi.astype(BF16), mid.astype(BF16), lo.astype(BF16)
 
 
-def fwd_kernel(heads, mem, queries, c, k_ref, ak_ref, vt_ref, qz_ref, aq_ref, o_ref, m_ref, l_ref, s_scr, mx_scr):
-    nq = queries // QT
-    n = heads * nq
-
-    def step(ia, sa, ib, sb):
-        if ia is not None:
-            h = ia // nq
-            qc = ia - h * nq
-            rhs = jnp.concatenate([qz_ref[pl.ds(pl.multiple_of(h * 128, 128), 128), pl.ds(pl.multiple_of(qc * QT, QT), QT)], aq_ref[...]], axis=0)
-            pair = pl.ds(pl.multiple_of((h // 2) * 128, 128), 128)
-            mx = None
-        if ib is not None:
-            hb = ib // nq
-            qb = ib - hb * nq
-            m = jnp.max(mx_scr[sb], axis=0, keepdims=True)
-            vrow = pl.ds(pl.multiple_of(hb * 64, 64), 64)
-            ls = None
-            acc = None
+RIGHT, LEFT = 0, 1
+
+class Ring:
+    def __init__(self, chips):
+        me = lax.axis_index('seq')
+        self.chips = chips
+        self.z = me // 2
+        self.core = me - 2 * self.z
+        self.partner = 2 * self.z + 1 - self.core
+        self.next = (2 * self.chip(1) + self.core, 2 * self.chip(-1) + self.core)
+
+    def chip(self, off):
+        return lax.rem(self.z + off + self.chips, self.chips)
+
+def remote(src, dst, ssem, rsem, dev):
+    return pltpu.make_async_remote_copy(src_ref=src, dst_ref=dst, send_sem=ssem, recv_sem=rsem, device_id={'seq': dev}, device_id_type=MESH)
+
+def enter(ring):
+    barrier = pltpu.get_barrier_semaphore()
+    for dev in (ring.partner, ring.next[0], ring.next[1]):
+        pl.semaphore_signal(barrier, inc=1, device_id={'seq': dev}, device_id_type=MESH)
+    pl.semaphore_wait(barrier, 3)
+
+def fwd_kernel(dims, y_ref, m_ref, ak_ref, wq_ref, wk_ref, wv_ref, g_ref,
+               yall_ref, att_ref, lse_ref,
+               yg, mg, wqt, k_s, vt_s, qz, s_scr, mx_scr, part, rbuf, own, pown,
+               agss, agrs, fss, frs, xss, xrs, rss, rrs):
+    chips, rows, mem, dim, hc, c = dims
+    QT = 2 * rows; T = 2 * mem; MC = min(256, mem); hh = hc // 2; inner = hc * 64
+    HR = hh * 64; half_chips = chips // 2
+    ring = Ring(chips); z = ring.z; core = ring.core
+    hops = {(RIGHT, 0): half_chips, (RIGHT, 1): half_chips - 1, (LEFT, 0): half_chips - 1, (LEFT, 1): half_chips}
+    sgn = (1, -1)
+    sub = rows // 2
+    enter(ring)
+
+    mine = pl.ds(pl.multiple_of(core * mem, mem), mem)
+    other = pl.ds(pl.multiple_of((1 - core) * mem, mem), mem)
+
+    def mcopy():
+        return remote(m_ref, mg, xss.at[0], xrs.at[0], ring.partner)
+
+    def ag_desc(d, s, t):
+        chip = ring.chip(-sgn[d] * (t - 1))
+        src = y_ref.at[pl.ds(s * sub, sub)] if t == 1 else yg.at[chip, core, s]
+        return remote(src, yg.at[chip, core, s], agss.at[d, s, t - 1], agrs.at[d, s, t - 1], ring.next[d])
+
+    def ag_recv(d, s, t):
+        slot = yg.at[ring.chip(-sgn[d] * t), core, s]
+        return remote(slot, slot, agss.at[d, s, t - 1], agrs.at[d, s, t - 1], ring.next[d])
+
+    def fw_desc(d, s, t):
+        slot = yg.at[ring.chip(-sgn[d] * t), core, s]
+        return remote(slot, slot, fss.at[d, s, t - 1], frs.at[d, s, t - 1], ring.partner)
+
+    def fw_recv(d, s, t):
+        slot = yg.at[ring.chip(-sgn[d] * t), 1 - core, s]
+        return remote(slot, slot, fss.at[d, s, t - 1], frs.at[d, s, t - 1], ring.partner)
+
+    def own_desc(s):
+        return remote(y_ref.at[pl.ds(s * sub, sub)], yg.at[z, core, s], xss.at[1 + s], xrs.at[1 + s], ring.partner)
+
+    def own_recv(s):
+        slot = yg.at[z, 1 - core, s]
+        return remote(slot, slot, xss.at[1 + s], xrs.at[1 + s], ring.partner)
+
+    def serve(t):
+        for d, s in ((RIGHT, 0), (LEFT, 1), (RIGHT, 1), (LEFT, 0)):
+            if hops[d, s] >= t:
+                ag_recv(d, s, t).wait_recv()
+                if hops[d, s] > t:
+                    ag_desc(d, s, t + 1).start()
+                fw_desc(d, s, t).start()
+
+    for d, s in ((RIGHT, 0), (LEFT, 1), (RIGHT, 1), (LEFT, 0)):
+        ag_desc(d, s, 1).start()
+    for s in range(2):
+        own_desc(s).start()
+    mcopy().start()
+    for s in range(2):
+        yg[z, core, s] = y_ref[s * sub:(s + 1) * sub, :]
+
+    hcol = pl.ds(pl.multiple_of(core * inner, 128), inner)
+    qz[...] = jnp.zeros_like(qz)
+    wqt[...] = wq_ref[:, hcol].T
+    wk = wk_ref[:, hcol]
+    wvt = wv_ref[:, hcol].T
+
+    def project(src, base):
         for j in range(mem // MC):
-            rows = slice(j * MC, (j + 1) * MC)
-            if ia is not None:
-                s = mm(jnp.concatenate([k_ref[rows, pair], ak_ref[rows, 0:16]], axis=1), rhs)
-                s_scr[sa, rows, :] = s
-                t = jnp.max(s.reshape(MC // 8, 8, QT), axis=0)
-                mx = t if mx is None else jnp.maximum(mx, t)
-            if ib is not None:
-                pr = jnp.exp2((s_scr[sb, rows, :] - m) * c)
-                t = jnp.sum(pr.reshape(MC // 8, 8, QT), axis=0)
-                ls = t if ls is None else ls + t
-                d = mm(vt_ref[vrow, rows], pr.astype(BF16))
-                acc = d if acc is None else acc + d
-        if ia is not None:
-            mx_scr[sa] = mx
-        if ib is not None:
-            qs = pl.ds(pl.multiple_of(qb * QT, QT), QT)
-            o_ref[vrow, qs] = acc
-            m_ref[pl.ds(hb, 1), qs] = m
-            l_ref[pl.ds(hb, 1), qs] = jnp.sum(ls, axis=0, keepdims=True)
-
-    step(0, 0, None, None)
+            r = pl.ds(pl.multiple_of(base + j * MC, MC), MC)
+            blk = src[j * MC:(j + 1) * MC, :]
+            k_s[r, :] = mm(blk, wk).astype(BF16)
+            vt_s[:, r] = mm_bt(wvt, blk).astype(BF16)
+
+    project(m_ref, core * mem)
+    serve(1)
+    mrecv = remote(mg, mg, xss.at[0], xrs.at[0], ring.partner)
+    mrecv.wait_recv()
+    project(mg, (1 - core) * mem)
+    serve(2)
+    gain = g_ref[...]
+
+    def stats(ref, hl):
+        return ref[HR + hl:HR + hl + 1, :], ref[HR + 8 + hl:HR + 9 + hl, :]
+
+    def flash(chip):
+        x = yg[chip].reshape(QT, dim).astype(F32)
+        n1 = rms_norm(x, gain).astype(BF16)
+        qt = mm_bt(wqt[...], n1).astype(BF16)
+        for h in range(hc):
+            lo = h * 128 + (h % 2) * 64
+            qz[lo:lo + 64, :] = qt[h * 64:(h + 1) * 64]
+        one_row = jnp.where(lax.broadcasted_iota(jnp.int32, (16, QT), 0) == 0, 1.0, 0.0).astype(BF16)
+
+        def step(h, slot, hp, pslot):
+            if h is not None:
+                rhs = jnp.concatenate([qz[pl.ds(pl.multiple_of(h * 128, 128), 128), :], one_row], axis=0)
+                pair = pl.ds(pl.multiple_of((h // 2) * 128, 128), 128)
+                mx = None
+            if hp is not None:
+                m = jnp.max(mx_scr[pslot], axis=0, keepdims=True)
+                vrow = pl.ds(pl.multiple_of(hp * 64, 64), 64)
+                ls = None
+                acc = None
+            for j in range(T // MC):
+                r = slice(j * MC, (j + 1) * MC)
+                if h is not None:
+                    s = mm(jnp.concatenate([k_s[r, pair], ak_ref[r, 0:16]], axis=1), rhs)
+                    s_scr[slot, r, :] = s
+                    t = jnp.max(s.reshape(MC // 8, 8, QT), axis=0)
+                    mx = t if mx is None else jnp.maximum(mx, t)
+                if hp is not None:
+                    pr = jnp.exp2((s_scr[pslot, r, :] - m) * c)
+                    t = jnp.sum(pr.reshape(MC // 8, 8, QT), axis=0)
+                    ls = t if ls is None else ls + t
+                    dd = mm(vt_s[vrow, r], pr.astype(BF16))
+                    acc = dd if acc is None else acc + dd
+            if h is not None:
+                mx_scr[slot] = mx
+            if hp is not None:
+                half = hp // hh
+                hl = hp - half * hh
+                part[chip, half, pl.ds(pl.multiple_of(hl * 64, 64), 64), :] = acc
+                part[chip, half, pl.ds(HR + hl, 1), :] = m
+                part[chip, half, pl.ds(HR + 8 + hl, 1), :] = jnp.sum(ls, axis=0, keepdims=True)
+
+        step(0, 0, None, None)
+        if hc > 2:
+            def pair_steps(i, carry):
+                step(2 * i + 1, 1, 2 * i, 0)
+                step(2 * i + 2, 0, 2 * i + 1, 1)
+                return carry
+            lax.fori_loop(0, hc // 2 - 1, pair_steps, 0)
+        step(hc - 1, 1, hc - 2, 0)
+        step(None, None, hc - 1, 1)
+
+    def merge(dst, src):
+        for hl in range(hh):
+            m1, l1 = stats(dst, hl)
+            m2, l2 = stats(src, hl)
+            m = jnp.maximum(m1, m2)
+            a = jnp.exp2((m1 - m) * c)
+            b = jnp.exp2((m2 - m) * c)
+            rr = slice(hl * 64, (hl + 1) * 64)
+            dst[rr, :] = dst[rr, :] * a + src[rr, :] * b
+            dst[HR + hl:HR + hl + 1, :] = m
+            dst[HR + 8 + hl:HR + 9 + hl, :] = l1 * a + l2 * b
+
+    def rs_desc(d, half, o):
+        chip = ring.chip(sgn[d] * o)
+        return remote(part.at[chip, half], rbuf.at[d, half, o - 1], rss.at[d, half, o - 1], rrs.at[d, half, o - 1], ring.next[d])
+
+    def rs_recv(d, half, o):
+        slot = rbuf.at[d, half, o]
+        return remote(slot, slot, rss.at[d, half, o], rrs.at[d, half, o], ring.next[d])
+
+    def rs_step(d, o):
+        for half in ((0, 1) if d == RIGHT else (1, 0)):
+            n = hops[d, half]
+            if o > n:
+                continue
+            if o < n:
+                rs_recv(d, half, o).wait_recv()
+                merge(part.at[ring.chip(sgn[d] * o), half], rbuf.at[d, half, o])
+            rs_desc(d, half, o).start()
+
+    order = [0, 1, half_chips]
+    for o in range(half_chips - 1, 1, -1):
+        order += [o, -o]
+    order += [-1]
+    n = len(order)
+
+    def ready(off):
+        if off == 0:
+            for s in range(2):
+                own_recv(s).wait_recv()
+            return
+        for s in range(2):
+            for d in (RIGHT, LEFT):
+                t = -off * sgn[d] if off != half_chips else half_chips
+                if 1 <= t <= hops[d, s] and (off == half_chips or t == abs(off)):
+                    fw_recv(d, s, t).wait_recv()
 
     def body(i, carry):
-        step(2 * i + 1, 1, 2 * i, 0)
-        step(jnp.minimum(2 * i + 2, n - 1), 0, 2 * i + 1, 1)
+        off = jnp.int32(order[-1])
+        for kk in range(n - 1):
+            off = jnp.where(i == kk, order[kk], off)
+        for kk in range(n):
+            @pl.when(i == kk)
+            def _(kk=kk):
+                if kk == 2:
+                    for t in range(3, half_chips + 1):
+                        serve(t)
+                ready(order[kk])
+        flash(ring.chip(off))
+        for kk in range(2, n):
+            @pl.when(i == kk)
+            def _(kk=kk):
+                o = order[kk]
+                if o == half_chips:
+                    rs_step(RIGHT, o); rs_step(LEFT, o)
+                elif o > 0:
+                    rs_step(RIGHT, o)
+                elif o == -2:
+                    rs_step(LEFT, 2); rs_step(RIGHT, 1)
+                else:
+                    rs_step(LEFT, -o)
         return carry
-
-    lax.fori_loop(0, n // 2, body, 0)
+    lax.fori_loop(0, n, body, 0)
+
+    for half in range(2):
+        for d in (RIGHT, LEFT):
+            rs_recv(d, half, 0).wait_recv()
+            merge(part.at[z, half], rbuf.at[d, half, 0])
+    for h in range(hc):
+        half, hl = h // hh, h % hh
+        m, l = stats(part.at[z, half], hl)
+        own[h * 64:(h + 1) * 64, :] = part[z, half, hl * 64:(hl + 1) * 64, :] / l
+        own[inner + h:inner + h + 1, :] = m + jnp.log2(l) / c
+    qmine = pl.ds(pl.multiple_of(core * rows, rows), rows)
+    qother = pl.ds(pl.multiple_of((1 - core) * rows, rows), rows)
+    xo = remote(own.at[:, qother], pown, xss.at[3], xrs.at[3], ring.partner)
+    xo.start()
+    yall_ref[...] = yg[...].reshape(chips * QT, dim)
+    hrow = pl.ds(pl.multiple_of(core * inner, inner), inner)
+    orow = pl.ds(pl.multiple_of((1 - core) * inner, inner), inner)
+    att_ref[hrow, :] = own[:inner, qmine]
+    lse_ref[core] = own[inner:inner + 8, qmine]
+    xo.wait()
+    att_ref[orow, :] = pown[:inner, :]
+    lse_ref[1 - core] = pown[inner:inner + 8, :]
+    mcopy().wait_send()
+    for s in range(2):
+        own_desc(s).wait_send()
+    for (d, s), nh in hops.items():
+        for t in range(1, nh + 1):
+            ag_desc(d, s, t).wait_send()
+            fw_desc(d, s, t).wait_send()
+            rs_desc(d, s, t).wait_send()
+
+def fwd_call(dims, y, memory, ak, wq, wk, wv, gain):
+    chips, rows, mem, dim, hc, c = dims
+    hh = hc // 2; inner = hc * 64; QT = 2 * rows; T = 2 * mem; HR = hh * 64; h2 = chips // 2
+    dma = pltpu.SemaphoreType.DMA
+    v = pl.BlockSpec(memory_space=VMEM)
+    return pl.pallas_call(
+        functools.partial(fwd_kernel, dims),
+        out_shape=(jax.ShapeDtypeStruct((chips * QT, dim), BF16), jax.ShapeDtypeStruct((2 * inner, rows), F32), jax.ShapeDtypeStruct((2, 8, rows), F32)),
+        in_specs=[v] * 7, out_specs=(v,) * 3,
+        scratch_shapes=[
+            VMEM((chips, 2, 2, rows // 2, dim), BF16), VMEM((mem, dim), BF16), VMEM((inner, dim), BF16),
+            VMEM((T, inner), BF16), VMEM((inner, T), BF16), VMEM((hc * 128, QT), BF16),
+            VMEM((2, T, QT), F32), VMEM((2, 8, QT), F32), VMEM((chips, 2, HR + 16, QT), F32), VMEM((2, 2, h2, HR + 16, QT), F32),
+            VMEM((inner + 8, QT), F32), VMEM((inner + 8, rows), F32),
+            dma((2, 2, h2)), dma((2, 2, h2)), dma((2, 2, h2)), dma((2, 2, h2)), dma((4,)), dma((4,)), dma((2, 2, h2)), dma((2, 2, h2))],
+        compiler_params=pltpu.CompilerParams(vmem_limit_bytes=60 * 1024 * 1024, collective_id=0, has_side_effects=True),
+        cost_estimate=pl.CostEstimate(flops=10**10, bytes_accessed=30 << 20, transcendentals=0),
+        name="attn_fwd")(y, memory, ak, wq, wk, wv, gain)
 
 
 def bwd_kernel(heads, mem, queries, c, k_ref, v_ref, ak_ref, kt_ref, qz_ref, aq_ref, doz_ref, ad_ref, dkt_ref, dvt_ref, dqt_ref):
@@ -166,8 +399,21 @@
         gain1 = norm_attn.astype(F32)
         gain2 = norm_mlp.astype(F32)
 
-        y_all = lax.all_gather(dec_in, 'seq', axis=0, tiled=True)
         go_all = lax.all_gather(grad_out.astype(BF16), 'seq', axis=0, tiled=True)
+        chips = group // 2
+        seq = lax.axis_index('seq')
+        lane = jnp.arange(128)
+
+        def aux_lanes(start, count):
+            pos = start + jnp.arange(count)
+            bias = jnp.where(pos < mem_len[0], 0.0, -1e30).astype(F32)
+            return jnp.where(lane[None, :] == 0, bias[:, None], jnp.where(lane[None, :] < 4, 1.0, 0.0)).astype(BF16)
+
+        y_all, att_t, lse2 = fwd_call((chips, rows, mem, dim, heads // 2, c), dec_in, memory, aux_lanes((seq // 2) * 2 * mem, 2 * mem),
+                                      wq2, wk2, wv2, gain1[None, :])
+        attended_f = att_t.T
+        attended = attended_f.astype(BF16)
+        lse = jnp.concatenate([lse2[0, :heads // 2], lse2[1, :heads // 2]], axis=0).T
         x_all = y_all.astype(F32)
         n1_all = rms_norm(x_all, gain1).astype(BF16)
         q_t = lax.dot_general(wq2, n1_all, (((0,), (1,)), ((), ())), preferred_element_type=F32).astype(BF16)
@@ -181,32 +427,7 @@
         mem_k = mm(memory, wk2).astype(BF16)
         mem_v = mm(memory, wv2).astype(BF16)
         k_t = mem_k.T
-        v_t = mem_v.T
-        pos = lax.axis_index('seq') * mem + jnp.arange(mem)
-        bias = jnp.where(pos < mem_len[0], 0.0, -1e30).astype(F32)
-        lane = jnp.arange(128)
-        ak = jnp.where(lane[None, :] == 0, bias[:, None], jnp.where(lane[None, :] < 4, 1.0, 0.0)).astype(BF16)
-        aq0 = jnp.where(jnp.arange(16)[:, None] == 0, 1.0, 0.0).astype(BF16) * jnp.ones((1, QT), BF16)
-
-        o_t, m_loc, l_loc = pl.pallas_call(
-            functools.partial(fwd_kernel, heads, mem, queries, c),
-            out_shape=(jax.ShapeDtypeStruct((inner, queries), F32), jax.ShapeDtypeStruct((heads, queries), F32), jax.ShapeDtypeStruct((heads, queries), F32)),
-            in_specs=vspec(5), out_specs=tuple(vspec(3)),
-            scratch_shapes=[VMEM((2, mem, QT), F32), VMEM((2, 8, QT), F32)],
-            compiler_params=params(),
-            cost_estimate=pl.CostEstimate(flops=4 * heads * mem * queries * 256, bytes_accessed=30 << 20, transcendentals=0),
-            name="attn_fwd")(mem_k, ak, v_t, qz, aq0)
-        m_all = lax.pmax(m_loc, 'seq')
-        scale_loc = jnp.exp2((m_loc - m_all) * c)
-        o_part = (o_t.reshape(heads, hd, queries) * scale_loc[:, None, :]).reshape(inner, queries).T
-        l_part = (l_loc * scale_loc).T
-        packed = jnp.concatenate([o_part, l_part, jnp.zeros((queries, 128 - heads), F32)], axis=1)
-        summed = lax.psum_scatter(packed, 'seq', scatter_dimension=0, tiled=True)
-        den = summed[:, inner:inner + heads]
-        attended_f = (summed[:, :inner].reshape(rows, heads, hd) / den[:, :, None]).reshape(rows, inner)
-        attended = attended_f.astype(BF16)
-        m_own = lax.dynamic_slice_in_dim(m_all, lax.axis_index('seq') * rows, rows, axis=1).T
-        lse = m_own + jnp.log2(den) / c
+        ak = aux_lanes(seq * mem, mem)
 
         x_in = dec_in.astype(F32)
         hidden = (x_in + mm(attended, wo2)).astype(BF16)

time: 693 us -> 529 us (0.76)
  waiting for transfers between devices: 331 us -> 121 us
  Pallas kernels: 121 us -> 169 us
  other arithmetic: 31.1 us -> 19.8 us
  local copies, waits for them, and re-layouts: 30.3 us -> 38.3 us
    pmax x1 -> x0, waiting for transfers between devices: 101 us -> none  [device_step(): m_all = lax.pmax(m_loc, 'seq')]
    reduce_scatter x1 -> x0, waiting for transfers between devices: 57.6 us -> none  [device_step(): summed = lax.psum_scatter(packed, 'seq', scatter_dimension=0, tiled=True)]
    pallas_call x1, Pallas kernels: 41.1 us -> 88.6 us  [fwd_call(): pl.pallas_call(functools.partial(fwd_kernel, dims), out_shape=(jax.ShapeD...]
    all_gather x1 -> x0, waiting for transfers between devices: 28 us -> none  [device_step(): y_all = lax.all_gather(dec_in, 'seq', axis=0, tiled=True)]
    all_gather x1, waiting for transfers between devices: 39.3 us -> 16.5 us  [device_step(): gathered = lax.all_gather(payload, 'seq', axis=0, tiled=False)]
    reshape x0 -> x3, local copies, waits for them, and re-layouts: none -> 7.15 us  [device_step(): wq2, wk2, wv2 = (w.reshape(dim, inner) for w in (wq, wk, wv))]
  transfers between devices with their start and end apart: 9 -> 6, of which waited for: 6 -> 3; matrix products, arithmetic and copies ran while one was open for 23% -> 31% of each run, Pallas kernels for 12% -> 15%
where the time goes in v2:
time: 529 us; the launch traced here: 522 us
  Pallas kernels  169 us (32%)
  matrix products  159 us (30%)
  waiting for transfers between devices  121 us (23%)
  local copies, waits for them, and re-layouts  38.3 us (7%)
  other arithmetic  19.8 us (4%)
  between operations  15.8 us (3%)
    pallas_call x1, Pallas kernels, fwd_call(): pl.pallas_call(functools.partial(fwd_kernel, dims), out_shape=(jax.ShapeD...  88.6 us
    pallas_call x1, Pallas kernels, device_step(): pl.pallas_call(functools.partial(bwd_kernel, heads, mem, queries, c), out...  79.9 us
    dot_general x5, matrix products, mm_at(): lax.dot_general(a, b, (((0,), (0,)), ((), ())), preferred_element_type=F32)  66.7 us
    psum x1, waiting for transfers between devices, device_step(): lax.psum(lax.dot_general(dkv, memory, (((1,), (0,)), ((), ())), preferred...  64.5 us
    dot_general x7, matrix products, mm(): return jnp.dot(a, b, preferred_element_type=F32)  38.2 us
    all_gather x1, waiting for transfers between devices, device_step(): dq_all = lax.all_gather(dq_b, 'seq', axis=0, tiled=True)  38 us
    dot_general x8, matrix products, mm_bt(): lax.dot_general(a, b, (((1,), (1,)), ((), ())), preferred_element_type=F32)  35.2 us
    all_gather x1, waiting for transfers between devices, device_step(): gathered = lax.all_gather(payload, 'seq', axis=0, tiled=False)  16.5 us
  transfers between devices with their start and end apart: 6, of which 3 were waited for; matrix products, arithmetic and copies ran while one was open for 31% of the time, Pallas kernels for 15%

profile of v2, /device:TPU:21, one launch (start us, length us, event | category | flops | bytes accessed | tf_op | source)
XLA Modules:
  0.0 522.2 jit_solution(211268729089455024)
XLA Ops:
  17.0 88.6 %attn_fwd.1 = (bf16[2048,768]{1,0:T(8,128)(2,1)}, f32[768,128]{1,0:T(8,128)}, f32[2,8,128]{2,1,0:T(8,128)}) custom-call(bf16[128,768]{1,0:T(8,128)(2,1)} %y_ref.1, bf16[1024,768]{1,0:T(8,128)(2,1)} %m_ref.1, bf16[2048,128]{1,0:T(8,128)(2,1)} %select_convert_fusion.ak_ref, bf16[768,768]{1,0:T(8,128)(2,1)} %copy.61.wq_ref, bf16[768,768]{1,0:T(8,128)(2,1)} %copy.62.wk_ref, ...), custom_call_target="tpu_custom_call" | custom-call | flops 10000000000 | bytes 31457280 | tf_op jit(solution)/shard_map/attn_fwd/pallas_call | solution.py:315
  109.8 4.1 fusion.68
  115.6 5.0 fusion.28
  120.6 4.6 multiply_reduce_fusion
  135.9 4.5 convolution_convert_fusion.3
  148.2 6.6 %convolution_convert_fusion.1 = bf16[2048,768]{0,1:T(8,128)(2,1)} fusion(bf16[768,768]{0,1:T(8,128)(2,1)} %bitcast.92, bf16[2048,768]{1,0:T(8,128)(2,1)} %get-tuple-element.18, f32[768]{0:T(1024)S(1)} %convert_element_type.147, f32[2048]{0:T(1024)S(1)} %add_rsqrt_fusion.1), kind=kOutput, calls=%fused_computation.29 | convolution fusion | flops 2423783424 | bytes 7482368 | tf_op jit(solution)/shard_map/dot_general | solution.py:419
  154.8 16.5 %all-gather.12.cloned.1.call-done = bf16[2304,896]{1,0:T(8,128)(2,1)} async-done(((bf16[144,896]{1,0:T(8,128)(2,1)}), bf16[2304,896]{1,0:T(8,128)(2,1)}) %all-gather.12.cloned.1.call-update) | async-done | bytes 4128784 | tf_op jit(solution)/shard_map/all_gather | solution.py:451
  175.9 4.0 convolution_convert_fusion
  186.9 5.0 pad_maximum_fusion.1
  193.6 79.9 %attn_bwd.1 = (f32[768,1024]{1,0:T(8,128)}, f32[768,1024]{1,0:T(8,128)}, f32[768,2048]{1,0:T(8,128)}) custom-call(bf16[1024,768]{1,0:T(8,128)(2,1)} %copy.75.k_ref, bf16[1024,768]{1,0:T(8,128)(2,1)} %convolution_convert_fusion.2.v_ref, bf16[1024,128]{1,0:T(8,128)(2,1)} %select_convert_fusion.1.ak_ref, bf16[768,1024]{1,0:T(8,128)(2,1)} %bitcast.104, ...), custom_call_target="tpu_custom_call" | custom-call | flops 64424509440 | bytes 41943040 | tf_op jit(solution)/shard_map/attn_bwd/pallas_call | solution.py:461
  273.6 7.9 %fusion.12 = (f32[2048]{0:T(1024)S(1)}, bf16[2048,768]{1,0:T(8,128)(2,1)}) fusion(bf16[2048,768]{0,1:T(8,128)(2,1)} %all-gather.8.cloned.1.call-done, bf16[768,768]{1,0:T(8,128)(2,1)} %bitcast.88, bf16[2048,768]{1,0:T(8,128)(2,1)} %get-tuple-element.18), kind=kOutput, calls=%fused_computation.20 | convolution fusion | flops 2425354240 | bytes 10625024 | tf_op jit(solution)/shard_map/dot_general | solution.py:21
  281.5 13.0 %fusion.70 = f32[2048,2048]{1,0:T(8,128)} fusion(bf16[2048,768]{1,0:T(8,128)(2,1)} %all-gather.10.cloned.1.call-done, bf16[2048,768]{1,0:T(8,128)(2,1)} %param.25), kind=kOutput, calls=%fused_computation.128 | convolution fusion | flops 6442450944 | bytes 23068672 | tf_op jit(solution)/shard_map/dot_general | solution.py:25
  294.6 9.9 %fusion.58 = f32[2048,2048]{1,0:T(8,128)} fusion(bf16[768,2048]{1,0:T(8,128)(2,1)S(1)} %copy-done, bf16[2048,768]{1,0:T(8,128)(2,1)S(1)} %copy-done.40, f32[768]{0:T(1024)S(1)} %convert_element_type.151, f32[2048]{0:T(1024)S(1)} %add_rsqrt_fusion), kind=kOutput, calls=%fused_computation.119 | convolution fusion | flops 6448742400 | bytes 23079936 | tf_op jit(solution)/shard_map/dot_general | solution.py:21
  304.5 10.0 %fusion.60 = f32[2048,2048]{1,0:T(8,128)} fusion(bf16[768,2048]{1,0:T(8,128)(2,1)S(1)} %copy-done.34, bf16[2048,768]{1,0:T(8,128)(2,1)S(1)} %copy-done.40, f32[768]{0:T(1024)S(1)} %convert_element_type.151, f32[2048]{0:T(1024)S(1)} %add_rsqrt_fusion), kind=kOutput, calls=%fused_computation.120 | convolution fusion | flops 6448742400 | bytes 23079936 | tf_op jit(solution)/shard_map/dot_general | solution.py:21
  314.5 21.7 %fusion.6 = f32[768,2048]{1,0:T(8,128)} fusion(f32[2048,2048]{1,0:T(8,128)} %fusion.58, f32[2048,2048]{1,0:T(8,128)} %fusion.70, f32[2048,2048]{1,0:T(8,128)} %fusion.60, bf16[2048,768]{1,0:T(8,128)(2,1)S(1)} %copy-done.40, f32[768]{0:T(1024)S(1)} %convert_element_type.151, f32[2048]{0:T(1024)S(1)} %add_rsqrt_fusion), kind=kOutput, calls=%fused_computation.13 | convolution fusion | flops 6494879744 | bytes 59780096 | tf_op jit(solution)/shard_map/dot_general | solution.py:29
  340.2 5.4 %convolution_bitcast_fusion = f32[768,1536]{0,1:T(8,128)} fusion(bf16[1024,768]{1,0:T(8,128)(2,1)S(1)} %copy-done.39, bf16[768,1024]{1,0:T(8,128)(2,1)S(1)} %convert_element_type.177, bf16[768,1024]{1,0:T(8,128)(2,1)S(1)} %multiply_convert_fusion.4), kind=kOutput, calls=%fused_computation.27 | convolution fusion | flops 2422210560 | bytes 9437184 | tf_op jit(solution)/shard_map/dot_general | solution.py:476
  347.5 16.5 %fusion.5 = f32[2048,768]{1,0:T(8,128)} fusion(bf16[2048,768]{1,0:T(8,128)(2,1)S(1)} %copy-done.36, f32[2048,2048]{1,0:T(8,128)} %fusion.60, f32[2048,2048]{1,0:T(8,128)} %fusion.58), kind=kOutput, calls=%fused_computation.12 | convolution fusion | flops 6467616768 | bytes 42991616 | tf_op jit(solution)/shard_map/dot_general | solution.py:29
  365.7 17.3 %fusion.4 = f32[768,2048]{1,0:T(8,128)} fusion(f32[2048,2048]{1,0:T(8,128)} %fusion.70, f32[2048,2048]{1,0:T(8,128)} %fusion.58, bf16[2048,768]{1,0:T(8,128)(2,1)} %get-tuple-element.59, f32[768]{0:T(1024)S(1)} %convert_element_type.151, f32[2048]{0:T(1024)S(1)} %add_rsqrt_fusion), kind=kOutput, calls=%fused_computation.11 | convolution fusion | flops 6473908224 | bytes 43002880 | tf_op jit(solution)/shard_map/dot_general | solution.py:29
  384.7 6.6 %fusion.19 = f32[1024,768]{1,0:T(8,128)} fusion(bf16[768,768]{0,1:T(8,128)(2,1)} %bitcast.111, bf16[768,768]{0,1:T(8,128)(2,1)} %bitcast.109, bf16[768,1024]{1,0:T(8,128)(2,1)S(1)} %copy-done.18, bf16[768,1024]{1,0:T(8,128)(2,1)} %copy-done.19), kind=kOutput, calls=%fused_computation.33 | convolution fusion | flops 2426929152 | bytes 8650752 | tf_op jit(solution)/shard_map/dot_general | solution.py:477
  391.3 4.0 fusion.69
  395.3 64.5 %all-reduce.3.cloned.1.call-done = f32[768,1536]{0,1:T(8,128)} async-done(((f32[768,1536]{0,1:T(8,128)}), f32[768,1536]{0,1:T(8,128)}) %all-reduce.3.cloned.1.call-update) | async-done | bytes 4718608 | tf_op jit(solution)/shard_map/psum | solution.py:476
  459.8 4.9 fusion.64
  466.1 38.0 %all-gather.6.cloned.1.call-done = bf16[2048,768]{0,1:T(8,128)(2,1)} async-done(((bf16[128,768]{0,1:T(8,128)(2,1)}), bf16[2048,768]{0,1:T(8,128)(2,1)}) %all-gather.6.cloned.1.call-update) | async-done | bytes 3145744 | tf_op jit(solution)/shard_map/all_gather | solution.py:472
  504.1 7.1 %fusion.29 = f32[768,768]{0,1:T(8,128)} fusion(bf16[2048,768]{0,1:T(8,128)(2,1)} %all-gather.6.cloned.1.call-done, bf16[2048,768]{1,0:T(8,128)(2,1)} %get-tuple-element.18, f32[768]{0:T(1024)S(1)} %copy-done.24, f32[2048]{0:T(1024)S(1)} %copy-done.27), kind=kOutput, calls=%fused_computation.53 | convolution fusion | flops 2422210560 | bytes 8662016 | tf_op jit(solution)/shard_map/dot_general | solution.py:29
  (163 shorter events, 60.8 us)
Async XLA Ops:
  7.2 106.8 %copy-start = (bf16[768,2048]{1,0:T(8,128)(2,1)S(1)}, bf16[768,2048]{1,0:T(8,128)(2,1)}, u32[]{:S(2)}) copy-start(bf16[768,2048]{1,0:T(8,128)(2,1)} %param.23) | copy-start | bytes 9437188
  7.2 164.1 %all-gather.12.cloned.1.call-start = ((), (), s32[]{:S(2)}) async-start(), calls=%async_computation.6 | async-start | bytes 4386816 | tf_op jit(solution)/shard_map/all_gather | solution.py:451
  7.3 8.6 %copy-start.29 = (bf16[128]{0:T(256)(128)(2,1)}, bf16[128]{0:T(256)(128)(2,1)S(1)}, u32[]{:S(2)}) copy-start(bf16[128]{0:T(256)(128)(2,1)S(1)} %compare_select_fusion) | copy-start | bytes 772
  7.3 8.6 %copy-start.31 = (pred[128]{0:T(512)(128)(4,1)}, pred[128]{0:T(512)(128)(4,1)S(1)}, u32[]{:S(2)}) copy-start(pred[128]{0:T(512)(128)(4,1)S(1)} %iota_compare_fusion.1) | copy-start | bytes 388
  8.1 7.2 %copy-start.25 = (bf16[768]{0:T(1024)(128)(2,1)S(1)}, bf16[768]{0:T(1024)(128)(2,1)}, u32[]{:S(2)}) copy-start(bf16[768]{0:T(1024)(128)(2,1)} %param.17) | copy-start | bytes 4612
  17.0 90.3 %copy-start.28 = (bf16[768]{0:T(1024)(128)(2,1)S(1)}, bf16[768]{0:T(1024)(128)(2,1)}, u32[]{:S(2)}) copy-start(bf16[768]{0:T(1024)(128)(2,1)} %param.22) | copy-start | bytes 4612
  17.0 90.3 %copy-start.15 = (f32[128,768]{1,0:T(8,128)S(1)}, f32[128,768]{1,0:T(8,128)}, u32[]{:S(2)}) copy-start(f32[128,768]{1,0:T(8,128)} %param.16) | copy-start | bytes 1179652
  134.1 139.5 %all-gather.8.cloned.1.call-start = ((), (), s32[]{:S(2)}) async-start(), calls=%async_computation.4 | async-start | bytes 3342336 | tf_op jit(solution)/shard_map/all_gather | solution.py:468
  135.0 146.6 %all-gather.10.cloned.1.call-start = ((), (), s32[]{:S(2)}) async-start(), calls=%async_computation.5 | async-start | bytes 3342336 | tf_op jit(solution)/shard_map/all_gather | solution.py:402
  135.8 228.2 %reduce-scatter.2.cloned.1.call-start = ((), (), s32[]{:S(2)}) async-start(), calls=%async_computation.1 | async-start | bytes 6684672 | tf_op jit(solution)/shard_map/reduce_scatter | solution.py:470
  135.8 12.4 %copy-start.23 = (f32[768]{0:T(1024)}, f32[768]{0:T(1024)S(1)}, u32[]{:S(2)}) copy-start(f32[768]{0:T(1024)S(1)} %convert_element_type.147) | copy-start | bytes 9220
  143.6 11.2 %copy-start.26 = (f32[2048]{0:T(1024)}, f32[2048]{0:T(1024)S(1)}, u32[]{:S(2)}) copy-start(f32[2048]{0:T(1024)S(1)} %add_rsqrt_fusion.1) | copy-start | bytes 24580
  273.5 186.3 %all-reduce.3.cloned.1.call-start = ((), (), s32[]{:S(2)}) async-start(), calls=%async_computation.3 | async-start | bytes 9437184 | tf_op jit(solution)/shard_map/psum | solution.py:476
  281.5 13.0 %copy-start.40 = (bf16[2048,768]{1,0:T(8,128)(2,1)S(1)}, bf16[2048,768]{1,0:T(8,128)(2,1)}, u32[]{:S(2)}) copy-start(bf16[2048,768]{1,0:T(8,128)(2,1)} %get-tuple-element.59) | copy-start | bytes 9437188
  294.6 9.9 %copy-start.34 = (bf16[768,2048]{1,0:T(8,128)(2,1)S(1)}, bf16[768,2048]{1,0:T(8,128)(2,1)}, u32[]{:S(2)}) copy-start(bf16[768,2048]{1,0:T(8,128)(2,1)} %param.24) | copy-start | bytes 9437188
  314.4 21.7 %copy-start.11 = (f32[768,1024]{1,0:T(8,128)S(1)}, f32[768,1024]{1,0:T(8,128)}, u32[]{:S(2)}) copy-start(f32[768,1024]{1,0:T(8,128)} %get-tuple-element.22) | copy-start | bytes 9437188
  345.7 158.4 %all-gather.6.cloned.1.call-start = ((), (), s32[]{:S(2)}) async-start(), calls=%async_computation.2 | async-start | bytes 3342336 | tf_op jit(solution)/shard_map/all_gather | solution.py:472
  365.7 18.9 %copy-start.18 = (bf16[768,1024]{1,0:T(8,128)(2,1)S(1)}, bf16[768,1024]{1,0:T(8,128)(2,1)}, u32[]{:S(2)}) copy-start(bf16[768,1024]{1,0:T(8,128)(2,1)} %copy-done.17) | copy-start | bytes 4718596
  395.3 69.4 %copy-start.4 = (bf16[768,12,64]{0,2,1:T(8,128)(2,1)S(1)}, bf16[768,12,64]{0,2,1:T(8,128)(2,1)}, u32[]{:S(2)}) copy-start(bf16[768,12,64]{0,2,1:T(8,128)(2,1)} %param.18) | copy-start | bytes 3538948
  395.3 69.4 %copy-start.12 = (bf16[128,768]{1,0:T(8,128)(2,1)S(1)}, bf16[128,768]{1,0:T(8,128)(2,1)}, u32[]{:S(2)}) copy-start(bf16[128,768]{1,0:T(8,128)(2,1)} %y_ref.1) | copy-start | bytes 589828
  395.3 69.4 %copy-start.14 = (bf16[128,768]{0,1:T(8,128)(2,1)S(1)}, bf16[128,768]{0,1:T(8,128)(2,1)}, u32[]{:S(2)}) copy-start(bf16[128,768]{0,1:T(8,128)(2,1)} %multiply_convert_fusion.7) | copy-start | bytes 589828
  395.3 69.4 %copy-start.24 = (f32[768]{0:T(1024)S(1)}, f32[768]{0:T(1024)}, u32[]{:S(2)}) copy-start(f32[768]{0:T(1024)} %copy-done.23) | copy-start | bytes 9220
  395.3 69.8 %copy-start.20 = (f32[128,768]{1,0:T(8,128)S(1)}, f32[128,768]{1,0:T(8,128)}, u32[]{:S(2)}) copy-start(f32[128,768]{1,0:T(8,128)} %get-tuple-element.28) | copy-start | bytes 1179652
  464.7 39.4 %copy-start.27 = (f32[2048]{0:T(1024)S(1)}, f32[2048]{0:T(1024)}, u32[]{:S(2)}) copy-start(f32[2048]{0:T(1024)} %copy-done.26) | copy-start | bytes 24580
  (23 other events, 92.8 us)
Sparse Core Ops, SparseCore 0:
  134.3 36.9 all-gather.11
  172.8 39.5 all-gather.7
  214.1 36.4 all-gather.9
  273.7 58.6 reduce-scatter.1
  345.8 113.9 all-reduce.2
  461.8 42.2 all-gather.5

commit v3 on v0

v3 whole, which is shorter than its diff:
```python
import functools
import math

import jax
import jax.numpy as jnp
from jax import lax
from jax.experimental import pallas as pl
from jax.experimental.pallas import tpu as pltpu
from jax.sharding import PartitionSpec as P

F32 = jnp.float32
BF16 = jnp.bfloat16
LOG2E = math.log2(math.e)
VMEM = pltpu.VMEM
MESH = pl.DeviceIdType.MESH


def mm(a, b):
    return jnp.dot(a, b, preferred_element_type=F32)


def mm_bt(a, b):
    return lax.dot_general(a, b, (((1,), (1,)), ((), ())), preferred_element_type=F32)


def mm_at(a, b):
    return lax.dot_general(a, b, (((0,), (0,)), ((), ())), preferred_element_type=F32)


def rms_norm(tensor, gain):
    mean_sq = jnp.mean(tensor * tensor, axis=-1, keepdims=True)
    return tensor * lax.rsqrt(mean_sq + 1e-6) * gain


def gated_unit(gate_pre, up_pre):
    return jax.nn.silu(gate_pre) * up_pre


RIGHT, LEFT = 0, 1
DMA = pltpu.SemaphoreType.DMA


class Ring:
    def __init__(self, chips):
        me = lax.axis_index('seq')
        self.chips = chips
        self.far = chips // 2
        self.z = me // 2
        self.core = me - 2 * self.z
        self.partner = 2 * self.z + 1 - self.core
        self.next = (2 * self.chip(1) + self.core, 2 * self.chip(-1) + self.core)
        self.hops = {(RIGHT, 0): self.far, (LEFT, 1): self.far, (RIGHT, 1): self.far - 1, (LEFT, 0): self.far - 1}

    def chip(self, off):
        return lax.rem(self.z + off + self.chips, self.chips)

    def ahead(self, d, k):
        return self.chip(k if d == RIGHT else -k)

    def enter(self):
        barrier = pltpu.get_barrier_semaphore()
        for dev in (self.partner,) + self.next:
            pl.semaphore_signal(barrier, inc=1, device_id={'seq': dev}, device_id_type=MESH)
        pl.semaphore_wait(barrier, 3)


def remote(src, dst, ssem, rsem, dev):
    return pltpu.make_async_remote_copy(src_ref=src, dst_ref=dst, send_sem=ssem, recv_sem=rsem, device_id={'seq': dev}, device_id_type=MESH)


class Share:
    def __init__(self, ring, buf, src, sems):
        self.ring, self.buf, self.src = ring, buf, src
        self.ss, self.rs = sems

    def slot(self, chip, half):
        return self.buf.at[chip, half]

    def send(self, d, half, t):
        slot = self.slot(self.ring.ahead(d, 1 - t), half)
        src = self.src(half) if t == 1 else slot
        return remote(src, slot, self.ss.at[d, half, t - 1], self.rs.at[d, half, t - 1], self.ring.next[d])

    def recv(self, d, half, t):
        slot = self.slot(self.ring.ahead(d, -t), half)
        return remote(slot, slot, self.ss.at[d, half, t - 1], self.rs.at[d, half, t - 1], self.ring.next[d])

    def start(self):
        for d, half in self.ring.hops:
            self.send(d, half, 1).start()

    def came(self, d, half, t):
        pass

    def serve(self, t):
        for (d, half), n in self.ring.hops.items():
            if t <= n:
                self.recv(d, half, t).wait_recv()
                if t < n:
                    self.send(d, half, t + 1).start()
                self.came(d, half, t)

    def drain(self):
        for (d, half), n in self.ring.hops.items():
            for t in range(1, n + 1):
                self.send(d, half, t).wait_send()


class Rows(Share):
    def __init__(self, ring, buf, src, sems):
        super().__init__(ring, buf, src, sems[:2])
        self.fs, self.fr, self.os, self.orr = sems[2:]

    def slot(self, chip, half):
        return self.buf.at[chip, self.ring.core, half]

    def pslot(self, chip, half):
        return self.buf.at[chip, 1 - self.ring.core, half]

    def start(self):
        super().start()
        for half in range(2):
            self.own(half).start()

    def own(self, half):
        return remote(self.src(half), self.slot(self.ring.z, half), self.os.at[half], self.orr.at[half], self.ring.partner)

    def forward(self, d, half, t):
        slot = self.slot(self.ring.ahead(d, -t), half)
        return remote(slot, slot, self.fs.at[d, half, t - 1], self.fr.at[d, half, t - 1], self.ring.partner)

    def came(self, d, half, t):
        self.forward(d, half, t).start()

    def ready(self, off):
        ring = self.ring
        if off == 0:
            for half in range(2):
                slot = self.pslot(ring.z, half)
                remote(slot, slot, self.os.at[half], self.orr.at[half], ring.partner).wait_recv()
            return
        for (d, half), n in ring.hops.items():
            t = ring.far if abs(off) == ring.far else (-off if d == RIGHT else off)
            if 1 <= t <= n:
                slot = self.pslot(ring.ahead(d, -t), half)
                remote(slot, slot, self.fs.at[d, half, t - 1], self.fr.at[d, half, t - 1], ring.partner).wait_recv()

    def drain(self):
        super().drain()
        for half in range(2):
            self.own(half).wait_send()
        for (d, half), n in self.ring.hops.items():
            for t in range(1, n + 1):
                self.forward(d, half, t).wait_send()


class Reduce:
    def __init__(self, ring, part, rbuf, merge, sems):
        self.ring, self.part, self.rbuf, self.merge = ring, part, rbuf, merge
        self.ss, self.rs = sems

    def send(self, d, half, o):
        return remote(self.part.at[self.ring.ahead(d, o), half], self.rbuf.at[d, half, o - 1], self.ss.at[d, half, o - 1], self.rs.at[d, half, o - 1], self.ring.next[d])

    def recv(self, d, half, o):
        slot = self.rbuf.at[d, half, o]
        return remote(slot, slot, self.ss.at[d, half, o], self.rs.at[d, half, o], self.ring.next[d])

    def step(self, d, o):
        for half in ((0, 1) if d == RIGHT else (1, 0)):
            n = self.ring.hops[d, half]
            if o > n:
                continue
            if o < n:
                self.recv(d, half, o).wait_recv()
                self.merge(self.part.at[self.ring.ahead(d, o), half], self.rbuf.at[d, half, o])
            self.send(d, half, o).start()

    def both(self, o):
        self.step(RIGHT, o)
        self.step(LEFT, o)

    def final(self):
        for half in range(2):
            for d in (RIGHT, LEFT):
                self.recv(d, half, 0).wait_recv()
                self.merge(self.part.at[self.ring.z, half], self.rbuf.at[d, half, 0])

    def drain(self):
        for (d, half), n in self.ring.hops.items():
            for o in range(1, n + 1):
                self.send(d, half, o).wait_send()


def pick(i, values):
    out = jnp.int32(values[-1])
    for k, v in enumerate(values[:-1]):
        out = jnp.where(i == k, jnp.int32(v), out)
    return out


def add_into(dst, src):
    dst[...] = dst[...] + src[...]


def parts3(x):
    hi = x.astype(BF16)
    rest = x - hi.astype(F32)
    mid = rest.astype(BF16)
    lo = (rest - mid.astype(F32)).astype(BF16)
    return hi, mid, lo


def bwd_kernel(dims, dh_ref, own_ref, gn_ref, att_ref, go_ref, k_ref, v_ref, kt_ref, qz_ref, ak_ref, ma_ref, mb_ref, y_ref, wo_ref, wq_ref, wk_ref, wv_ref, g1_ref,
               gmem_ref, gwkv_ref, gwq_ref, gvec_ref, dqo_ref, attg, gog, dho,
               dhg, doz, aqs, ads, stb, dk, dv, dkv, dkvp, dqp, dqr, dqa, arp, arr, ara, pvec, pdq, spb,
               *sems):
    chips, rows, mem, dim, hc, c = dims
    QT = 2 * rows
    T = 2 * mem
    MC = min(256, mem)
    nm = T // MC
    inner = hc * 64
    np_ = hc // 2
    seg = 256 // chips // 2
    ring = Ring(chips)
    z, core, far = ring.z, ring.core, ring.far
    sems = list(sems)

    def take(n):
        out = sems[:n]
        del sems[:n]
        return out

    half_rows = rows // 2
    rsrc = lambda ref: (lambda half: ref.at[pl.ds(half * half_rows, half_rows)])
    dh_g = Rows(ring, dhg, rsrc(dh_ref), take(6))
    att_g = Rows(ring, attg, rsrc(att_ref), take(6))
    go_g = Rows(ring, gog, rsrc(go_ref), take(6))
    st_g = Share(ring, stb, lambda half: stb.at[z, half], take(2))
    dq_r = [Reduce(ring, dqp.at[p], dqr.at[p], add_into, take(2)) for p in range(np_)]
    dq_s = [Share(ring, dqa.at[p], lambda half, p=p: dqa.at[p, z, half], take(2)) for p in range(np_)]
    ar_r = [Reduce(ring, arp.at[p], arr.at[p], add_into, take(2)) for p in range(np_)]
    ar_s = [Share(ring, ara.at[p], lambda half, p=p: ara.at[p, z, half], take(2)) for p in range(np_)]
    xs, xr, ls = take(3)
    ring.enter()
    dh_g.start()
    locals_ = []
    for n, (ref, buf) in enumerate(((att_ref, attg), (go_ref, gog))):
        for half in range(2):
            cp = pltpu.make_async_copy(ref.at[pl.ds(half * half_rows, half_rows)], buf.at[z, core, half], ls.at[2 * n + half])
            cp.start()
            locals_.append(cp)
    for half in range(2):
        dhg[z, core, half] = dh_ref[half * half_rows:(half + 1) * half_rows, :]
    doz[...] = jnp.zeros_like(doz)
    hrow = pl.ds(pl.multiple_of(core * inner, inner), inner)
    orow = pl.ds(pl.multiple_of((1 - core) * inner, inner), inner)
    wo_h = wo_ref[hrow, :]

    def d_out(chip):
        return mm_bt(wo_h, dhg[chip].reshape(QT, dim))

    def lanes(chip):
        return pl.ds(pl.multiple_of(chip * QT, QT), QT)

    def prepare(chip, dot=None):
        dot = d_out(chip) if dot is None else dot
        dob = dot.astype(BF16)
        q = lanes(chip)
        row = lax.broadcasted_iota(jnp.int32, (16, QT), 0)
        for h in range(hc):
            lo = h * 128 + (h % 2) * 64
            doz[lo:lo + 64, q] = dob[h * 64:(h + 1) * 64]
            for ref, half, first in ((aqs, 0, 1.0), (ads, 1, 0.0)):
                a, b, e = (x.astype(F32) for x in parts3(stb[chip, half, h:h + 1, :]))
                ref[h * 16:(h + 1) * 16, q] = jnp.where(row == 0, first, jnp.where(row == 1, a, jnp.where(row == 2, b, jnp.where(row == 3, e, 0.0)))).astype(BF16)

    dh_g.ready(0)
    dot0 = d_out(z)
    prod = dot0 * own_ref[:inner, :]
    for h in range(hc):
        stb[z, 0, h:h + 1, :] = -own_ref[inner + h:inner + h + 1, :]
        stb[z, 1, h:h + 1, :] = -jnp.sum(prod[h * 64:(h + 1) * 64], axis=0, keepdims=True)
    stb[z, 0, hc:8, :] = gn_ref[0:8 - hc, :]
    stb[z, 1, hc:8, :] = gn_ref[8 - hc:16 - 2 * hc, :]
    st_g.start()
    prepare(z, dot0)

    def tile(h, chip, p, hl):
        q = lanes(chip)
        hz = pl.ds(pl.multiple_of(h * 128, 128), 128)
        h16 = pl.ds(pl.multiple_of(h * 16, 16), 16)
        ps = slice(p * 128, (p + 1) * 128)
        hr = pl.ds(pl.multiple_of(hl * 64, 64), 64)
        hz64 = pl.ds(pl.multiple_of(h * 128 + hl * 64, 64), 64)
        h64 = pl.ds(pl.multiple_of(h * 64, 64), 64)
        q_t = qz_ref[hz64, q]
        do_t = doz[hz64, q]
        r1 = jnp.concatenate([qz_ref[hz, q], aqs[h16, q]], axis=0)
        r2 = jnp.concatenate([doz[hz, q], ads[h16, q]], axis=0)
        stage = {}
        dq = None
        for j in range(nm + 2):
            if j < nm:
                r = slice(j * MC, (j + 1) * MC)
                ak = ak_ref[r, 0:16]
                stage["a", j] = (mm(jnp.concatenate([k_ref[r, ps], ak], axis=1), r1), mm(jnp.concatenate([v_ref[r, ps], ak], axis=1), r2))
            if 1 <= j <= nm:
                s, dp = stage.pop(("a", j - 1))
                a = jnp.exp2(s * c)
                stage["b", j - 1] = (a.astype(BF16), (a * dp).astype(BF16))
            if j >= 2:
                r = slice((j - 2) * MC, (j - 1) * MC)
                pb, ds = stage.pop(("b", j - 2))
                dv[hr, r] += mm_bt(do_t, pb)
                dk[hr, r] += mm_bt(q_t, ds)
                d = mm(kt_ref[h64, r], ds)
                dq = d if dq is None else dq + d
        dqp[p, chip, hl] = dq

    near = [0]
    for o in range(1, far):
        near += [o, -o]
    near += [far]
    far_first = [far] + [s * o for o in range(far - 1, 0, -1) for s in (1, -1)] + [0]
    scale = 0.125

    def run_pair(p, order, before, after):
        dk[...] = jnp.zeros_like(dk)
        dv[...] = jnp.zeros_like(dv)

        def body(i, carry):
            chip = ring.chip(pick(i, order))
            for kk, fn in sorted(before.items()):
                pl.when(i == kk)(functools.partial(fn, chip))
            lax.fori_loop(0, 2, lambda hl, cc: (tile(2 * p + hl, chip, p, hl), cc)[1], 0)
            for kk, fn in sorted(after.items()):
                pl.when(i == kk)(fn)
            return carry

        lax.fori_loop(0, chips, body, 0)
        dkb = (dk[...] * scale).astype(BF16)
        dvb = dv[...].astype(BF16)
        dkv[p, 0:128, :] = dkb
        dkv[p, 128:256, :] = dvb
        xp(p).start()
        for part in range(2):
            mine = pl.ds(pl.multiple_of(core * mem, mem), mem)
            other = pl.ds(pl.multiple_of((1 - core) * mem, mem), mem)
            g = mm(dkv[p, part * 128:(part + 1) * 128, mine], ma_ref[...]) + mm(dkv[p, part * 128:(part + 1) * 128, other], mb_ref[...])
            for n in range(128 // seg):
                row = part * 128 + n * seg
                arp[p, row // (2 * seg), (row // seg) % 2] = g[n * seg:(n + 1) * seg]

    other_cols = pl.ds(pl.multiple_of((1 - core) * mem, mem), mem)
    my_cols = pl.ds(pl.multiple_of(core * mem, mem), mem)

    def xp(p):
        return remote(dkv.at[p, :, other_cols], dkvp.at[p], xs.at[p], xr.at[p], ring.partner)

    def gate(off, t=None):
        def fn(chip):
            if t is not None:
                dh_g.serve(t)
                st_g.serve(t)
            dh_g.ready(off)
            prepare(chip)
        return fn

    before0 = {}
    for n, off in enumerate(near):
        if off:
            before0[n] = gate(off, abs(off) if off > 0 else None)
    run_pair(0, near, before0, {})

    def seq(*fns):
        def run(*_):
            for f in fns:
                f()
        return run

    part_ = functools.partial
    def bg_reduce(p, base):
        ev = {}
        for n, o in enumerate(range(far, 0, -1)):
            ev.setdefault(2 * n, []).extend([part_(dq_r[p].both, o), part_(ar_r[p].both, o)])
        return ev

    def finish_reduce(p):
        dq_r[p].final()
        ar_r[p].final()
        for half in range(2):
            dqa[p, z, half] = (dqp[p, z, half] * scale).astype(BF16)
            ara[p, z, half] = arp[p, z, half]
        dq_s[p].start()
        ar_s[p].start()
        xq(p).start()

    qother = pl.ds(pl.multiple_of((1 - core) * rows, rows), rows)

    def xq(p):
        return remote(dqa.at[p, z, :, :, qother], pdq.at[p], xs.at[np_ + p], xr.at[np_ + p], ring.partner)

    def merged(*evs):
        out = {}
        for ev in evs:
            for kk, fns in ev.items():
                out.setdefault(kk, []).extend(fns)
        return {kk: seq(*fns) for kk, fns in out.items()}

    def spread(g):
        return {2 * t - 1: [part_(g.serve, t)] for t in range(1, far + 1)}

    cp = pltpu.make_async_copy(dhg, dho, ls.at[4])
    cp.start()
    locals_.append(cp)
    att_g.start()
    run_pair(1, far_first, {}, merged(bg_reduce(0, 0), spread(att_g)))
    finish_reduce(0)
    go_g.start()
    tail = {0: [part_(dq_s[0].serve, 1), part_(ar_s[0].serve, 1)], 2: [part_(dq_s[0].serve, 2), part_(ar_s[0].serve, 2)], 4: [part_(dq_s[0].serve, 3), part_(ar_s[0].serve, 3)], 6: [part_(dq_s[0].serve, 4), part_(ar_s[0].serve, 4)]}
    inl = {}
    for n, off in enumerate(far_first):
        if off == far:
            inl[n] = [part_(dq_r[2].both, far)]
        elif off > 0:
            inl[n] = [part_(dq_r[2].step, RIGHT, off)]
        elif off < 0:
            inl[n] = [part_(dq_r[2].step, LEFT, -off)]
    run_pair(2, far_first, {}, merged(bg_reduce(1, 0), tail, spread(go_g), inl))
    finish_reduce(1)
    ar_r[2].both(far)
    dq_r[2].final()
    for half in range(2):
        dqa[2, z, half] = (dqp[2, z, half] * scale).astype(BF16)
    dq_s[2].start()
    xq(2).start()
    for p in range(np_):
        remote(dkvp.at[p], dkvp.at[p], xs.at[p], xr.at[p], ring.partner).wait_recv()
    step_fns = [[part_(ar_r[2].both, 3), part_(dq_s[1].serve, 1), part_(ar_s[1].serve, 1), part_(dq_s[2].serve, 1)],
                [part_(ar_r[2].both, 2), part_(dq_s[1].serve, 2), part_(ar_s[1].serve, 2), part_(dq_s[2].serve, 2)],
                [part_(ar_r[2].both, 1), part_(dq_s[1].serve, 3), part_(ar_s[1].serve, 3), part_(dq_s[2].serve, 3)],
                [part_(dq_s[1].serve, 4), part_(ar_s[1].serve, 4), part_(dq_s[2].serve, 4)]]
    nb = 4
    for b in range(nb):
        w = mem // nb
        cb = pl.ds(pl.multiple_of(core * mem + b * w, w), w)
        acc = None
        for p in range(np_):
            for part, w_ref in ((0, wk_ref), (1, wv_ref)):
                own_cols = pl.ds(pl.multiple_of(core * inner + p * 128, 128), 128)
                oth_cols = pl.ds(pl.multiple_of((1 - core) * inner + p * 128, 128), 128)
                e = slice(part * 128, (part + 1) * 128)
                d = mm(jnp.concatenate([w_ref[:, own_cols], w_ref[:, oth_cols]], axis=1),
                       jnp.concatenate([dkv[p, e, cb], dkvp[p, e, b * w:(b + 1) * w]], axis=0))
                acc = d if acc is None else acc + d
        gmem_ref[b * w:(b + 1) * w, :] = acc.T
        for f in step_fns[b]:
            f()
    ar_r[2].final()
    for half in range(2):
        ara[2, z, half] = arp[2, z, half]
    ar_s[2].start()
    gain = g1_ref[...]
    wqt = wq_ref[:, pl.ds(pl.multiple_of(core * inner, 128), inner)].T
    gvec = jnp.zeros((1, dim), F32)
    gvec2 = jnp.zeros((16 - 2 * hc, QT), F32)
    for ch in range(chips):
        x = y_ref[ch * QT:(ch + 1) * QT, :].astype(F32)
        xhat = x * lax.rsqrt(jnp.mean(x * x, axis=-1, keepdims=True) + 1e-6)
        n1 = (xhat * gain).astype(BF16)
        dqc = jnp.concatenate([dqa[p, ch].reshape(128, QT) for p in range(np_)], axis=0)
        dn = mm_at(dqc, wqt)
        d = mm(dqc, n1)
        if ch == 0:
            gwq_ref[core] = d
        else:
            gwq_ref[core] += d
        gvec = gvec + jnp.sum(dn * xhat, axis=0, keepdims=True)
        gvec2 = gvec2 + jnp.concatenate([stb[ch, 0, hc:8, :], stb[ch, 1, hc:8, :]], axis=0)
        if ch % 2 == 1:
            ar_s[2].serve(ch // 2 + 1)
    spb[0:1, :] = gvec
    for n in range(dim // QT):
        spb[1:2, n * QT:(n + 1) * QT] = gvec2[n:n + 1]
    cv = remote(spb, pvec, xs.at[2 * np_], xr.at[2 * np_], ring.partner)
    cq = remote(gwq_ref.at[core], gwq_ref.at[core], xs.at[2 * np_ + 1], xr.at[2 * np_ + 1], ring.partner)
    cv.start()
    cq.start()
    for p in range(np_):
        gwkv_ref[core, p] = ara[p]
    cw = [remote(ara.at[p], gwkv_ref.at[core, p], xs.at[2 * np_ + 2 + p], xr.at[2 * np_ + 2 + p], ring.partner) for p in range(np_)]
    for p in range(np_):
        cw[p].start()
    qmine = pl.ds(pl.multiple_of(core * rows, rows), rows)
    for p in range(np_):
        own_r = pl.ds(pl.multiple_of(core * inner + p * 128, 128), 128)
        oth_r = pl.ds(pl.multiple_of((1 - core) * inner + p * 128, 128), 128)
        dqo_ref[own_r, :] = dqa[p, z, :, :, qmine].reshape(128, rows)
        xq(p).wait()
        dqo_ref[oth_r, :] = pdq[p].reshape(128, rows)
    cv.wait()
    gvec_ref[...] = spb[0:2] + pvec[0:2]
    cq.wait()
    for p in range(np_):
        cw[p].wait()
        xp(p).wait_send()
    for g in (att_g, go_g):
        for off in near:
            g.ready(off)
    for cp in locals_:
        cp.wait()
    for obj in [dh_g, att_g, go_g, st_g] + dq_r + dq_s + ar_r + ar_s:
        obj.drain()


def bwd_call(dims, *args):
    chips, rows, mem, dim, hc, c = dims
    inner = hc * 64
    QT = 2 * rows
    T = 2 * mem
    np_ = hc // 2
    h2 = chips // 2
    seg = 256 // chips // 2
    v = pl.BlockSpec(memory_space=VMEM)
    hbm = pl.BlockSpec(memory_space=pl.ANY)
    s3 = (2, 2, h2)
    rows_sems = [DMA(s3)] * 4 + [DMA((2,))] * 2
    two = [DMA(s3)] * 2
    S = jax.ShapeDtypeStruct
    gshape = (chips, 2, 2, rows // 2, dim)
    return pl.pallas_call(
        functools.partial(bwd_kernel, dims),
        out_shape=(S((mem, dim), F32), S((2, np_, chips, 2, seg, dim), F32), S((2, inner, dim), F32), S((2, dim), F32), S((2 * inner, rows), BF16), S(gshape, BF16), S(gshape, BF16), S(gshape, BF16)),
        in_specs=[v] * 18, out_specs=(v,) * 5 + (hbm,) * 3,
        scratch_shapes=[
            VMEM(gshape, BF16), VMEM((hc * 128, chips * QT), BF16), VMEM((hc * 16, chips * QT), BF16), VMEM((hc * 16, chips * QT), BF16),
            VMEM((chips, 2, 8, QT), F32), VMEM((128, T), F32), VMEM((128, T), F32), VMEM((np_, 256, T), BF16), VMEM((np_, 256, mem), BF16),
            VMEM((np_, chips, 2, 64, QT), F32), VMEM((np_, 2, 2, h2, 64, QT), F32), VMEM((np_, chips, 2, 64, QT), BF16),
            VMEM((np_, chips, 2, seg, dim), F32), VMEM((np_, 2, 2, h2, seg, dim), F32), VMEM((np_, chips, 2, seg, dim), F32),
            VMEM((8, dim), F32), VMEM((np_, 2, 64, rows), BF16), VMEM((8, dim), F32)]
        + rows_sems * 3 + two * (1 + 4 * np_) + [DMA((3 * np_ + 2,))] * 2 + [DMA((5,))],
        compiler_params=pltpu.CompilerParams(vmem_limit_bytes=66_900_000, collective_id=1, has_side_effects=True),
        cost_estimate=pl.CostEstimate(flops=10**10, bytes_accessed=30 << 20, transcendentals=0),
        name="attn_bwd")(*args)

def fwd_kernel(dims, y_ref, m_ref, ak_ref, wq_ref, wk_ref, wv_ref, g_ref,
               own, att_ref, k_s, v_s, kt_s, qz, mg, yall,
               yg, wqt, vt_s, s_scr, mx_scr, part, rbuf, patt, satt, *sems):
    chips, rows, mem, dim, hc, c = dims
    QT = 2 * rows
    T = 2 * mem
    MC = min(256, mem)
    hh = hc // 2
    inner = hc * 64
    HR = hh * 64
    ring = Ring(chips)
    z, core, far = ring.z, ring.core, ring.far
    sub = rows // 2
    xs, xr, ls = sems[8:]
    y_g = Rows(ring, yg, lambda half: y_ref.at[pl.ds(half * sub, sub)], sems[:6])

    def merge(dst, src):
        for hl in range(hh):
            mr = slice(HR + hl, HR + hl + 1)
            lr = slice(HR + 8 + hl, HR + 9 + hl)
            m1, m2 = dst[mr, :], src[mr, :]
            m = jnp.maximum(m1, m2)
            a = jnp.exp2((m1 - m) * c)
            b = jnp.exp2((m2 - m) * c)
            rr = slice(hl * 64, (hl + 1) * 64)
            dst[rr, :] = dst[rr, :] * a + src[rr, :] * b
            dst[mr, :] = m
            dst[lr, :] = dst[lr, :] * a + src[lr, :] * b

    o_r = Reduce(ring, part, rbuf, merge, sems[6:8])
    ring.enter()
    y_g.start()
    mx_copy = remote(m_ref, mg, xs.at[0], xr.at[0], ring.partner)
    mx_copy.start()
    for half in range(2):
        yg[z, core, half] = y_ref[half * sub:(half + 1) * sub, :]
    hcol = pl.ds(pl.multiple_of(core * inner, 128), inner)
    qz[...] = jnp.zeros_like(qz)
    wqt[...] = wq_ref[:, hcol].T
    wk = wk_ref[:, hcol]
    wv = wv_ref[:, hcol]

    def project(src, base):
        for j in range(mem // MC):
            r = pl.ds(pl.multiple_of(base + j * MC, MC), MC)
            blk = src[j * MC:(j + 1) * MC, :]
            kb = mm(blk, wk).astype(BF16)
            vb = mm(blk, wv).astype(BF16)
            k_s[r, :] = kb
            v_s[r, :] = vb
            kt_s[:, r] = kb.T
            vt_s[:, r] = vb.T

    project(m_ref, core * mem)
    y_g.serve(1)
    mx_copy.wait_recv()
    project(mg, (1 - core) * mem)
    y_g.serve(2)
    gain = g_ref[...]

    def flash(chip):
        x = yg[chip].reshape(QT, dim).astype(F32)
        n1 = rms_norm(x, gain).astype(BF16)
        qt = mm_bt(wqt[...], n1).astype(BF16)
        q = pl.ds(pl.multiple_of(chip * QT, QT), QT)
        for h in range(hc):
            lo = h * 128 + (h % 2) * 64
            qz[lo:lo + 64, q] = qt[h * 64:(h + 1) * 64]
        one_row = jnp.where(lax.broadcasted_iota(jnp.int32, (16, QT), 0) == 0, 1.0, 0.0).astype(BF16)

        def step(h, slot, hp, pslot):
            if h is not None:
                rhs = jnp.concatenate([qz[pl.ds(pl.multiple_of(h * 128, 128), 128), q], one_row], axis=0)
                pair = pl.ds(pl.multiple_of((h // 2) * 128, 128), 128)
                mx = None
            if hp is not None:
                m = jnp.max(mx_scr[pslot], axis=0, keepdims=True)
                vrow = pl.ds(pl.multiple_of(hp * 64, 64), 64)
                ls_ = None
                acc = None
            for j in range(T // MC):
                r = slice(j * MC, (j + 1) * MC)
                if h is not None:
                    s = mm(jnp.concatenate([k_s[r, pair], ak_ref[r, 0:16]], axis=1), rhs)
                    s_scr[slot, r, :] = s
                    t = jnp.max(s.reshape(MC // 8, 8, QT), axis=0)
                    mx = t if mx is None else jnp.maximum(mx, t)
                if hp is not None:
                    pr = jnp.exp2((s_scr[pslot, r, :] - m) * c)
                    t = jnp.sum(pr.reshape(MC // 8, 8, QT), axis=0)
                    ls_ = t if ls_ is None else ls_ + t
                    dd = mm(vt_s[vrow, r], pr.astype(BF16))
                    acc = dd if acc is None else acc + dd
            if h is not None:
                mx_scr[slot] = mx
            if hp is not None:
                half = hp // hh
                hl = hp - half * hh
                part[chip, half, pl.ds(pl.multiple_of(hl * 64, 64), 64), :] = acc
                part[chip, half, pl.ds(HR + hl, 1), :] = m
                part[chip, half, pl.ds(HR + 8 + hl, 1), :] = jnp.sum(ls_, axis=0, keepdims=True)

        step(0, 0, None, None)
        if hc > 2:
            def pair_steps(i, carry):
                step(2 * i + 1, 1, 2 * i, 0)
                step(2 * i + 2, 0, 2 * i + 1, 1)
                return carry
            lax.fori_loop(0, hc // 2 - 1, pair_steps, 0)
        step(hc - 1, 1, hc - 2, 0)
        step(None, None, hc - 1, 1)

    order = [0, 1, far]
    for o in range(far - 1, 1, -1):
        order += [o, -o]
    order += [-1]

    def body(i, carry):
        for kk, off in enumerate(order):
            def get(kk=kk, off=off):
                if kk == 2:
                    for t in range(3, far + 1):
                        y_g.serve(t)
                y_g.ready(off)
            pl.when(i == kk)(get)
        flash(ring.chip(pick(i, order)))
        for kk, off in enumerate(order):
            if kk < 2:
                continue
            def put(off=off):
                if off == far:
                    o_r.both(far)
                elif off > 0:
                    o_r.step(RIGHT, off)
                else:
                    o_r.step(LEFT, -off)
                    if off == -2:
                        o_r.step(RIGHT, 1)
            pl.when(i == kk)(put)
        return carry

    lax.fori_loop(0, chips, body, 0)
    yc = pltpu.make_async_copy(yg, yall, ls.at[0])
    yc.start()
    o_r.final()
    qmine = pl.ds(pl.multiple_of(core * rows, rows), rows)
    qother = pl.ds(pl.multiple_of((1 - core) * rows, rows), rows)
    for h in range(hc):
        half, hl = h // hh, h % hh
        m = part[z, half, HR + hl:HR + hl + 1, :]
        l = part[z, half, HR + 8 + hl:HR + 9 + hl, :]
        o = part[z, half, hl * 64:(hl + 1) * 64, :] / l
        own[h * 64:(h + 1) * 64, :] = o
        own[inner + h:inner + h + 1, :] = m + jnp.log2(l) / c
    satt[...] = own[:inner, qother].astype(BF16)
    xo = remote(satt, patt, xs.at[1], xr.at[1], ring.partner)
    xo.start()
    att_ref[pl.ds(pl.multiple_of(core * inner, inner), inner), :] = own[:inner, qmine].astype(BF16)
    xo.wait()
    att_ref[pl.ds(pl.multiple_of((1 - core) * inner, inner), inner), :] = patt[...]
    mx_copy.wait_send()
    yc.wait()
    y_g.drain()
    o_r.drain()


def fwd_call(dims, *args):
    chips, rows, mem, dim, hc, c = dims
    hh = hc // 2
    inner = hc * 64
    QT = 2 * rows
    T = 2 * mem
    HR = hh * 64
    h2 = chips // 2
    v = pl.BlockSpec(memory_space=VMEM)
    S = jax.ShapeDtypeStruct
    s3 = (2, 2, h2)
    gshape = (chips, 2, 2, rows // 2, dim)
    return pl.pallas_call(
        functools.partial(fwd_kernel, dims),
        out_shape=(S((inner + 8, QT), F32), S((2 * inner, rows), BF16), S((T, inner), BF16), S((T, inner), BF16), S((inner, T), BF16),
                   S((hc * 128, chips * QT), BF16), S((mem, dim), BF16), S(gshape, BF16)),
        in_specs=[v] * 7, out_specs=(v,) * 7 + (pl.BlockSpec(memory_space=pl.ANY),),
        scratch_shapes=[
            VMEM(gshape, BF16), VMEM((inner, dim), BF16), VMEM((inner, T), BF16), VMEM((2, T, QT), F32), VMEM((2, 8, QT), F32),
            VMEM((chips, 2, HR + 16, QT), F32), VMEM((2, 2, h2, HR + 16, QT), F32), VMEM((inner, rows), BF16), VMEM((inner, rows), BF16)]
        + [DMA(s3)] * 4 + [DMA((2,))] * 2 + [DMA(s3)] * 2 + [DMA((2,))] * 2 + [DMA((1,))],
        compiler_params=pltpu.CompilerParams(vmem_limit_bytes=62 * 1024 * 1024, collective_id=0, has_side_effects=True),
        cost_estimate=pl.CostEstimate(flops=10**10, bytes_accessed=30 << 20, transcendentals=0),
        name="attn_fwd")(*args)

def solution(mesh):
    group = mesh.shape['seq']
    row_spec = P(('data', 'seq'), None)
    part_vec = P('data')
    part_mat = P('data', None)
    part_cube = P('data', None, None)

    def device_step(dec_in, memory, mem_len, grad_out, norm_attn, wq, wk, wv, wo, norm_mlp, w_gate, w_up, w_down):
        rows, dim = dec_in.shape
        mem = memory.shape[0]
        heads, hd = wq.shape[1], wq.shape[2]
        inner = heads * hd
        queries = rows * group
        chips = group // 2
        hc = heads // 2
        c = LOG2E * hd ** -0.5
        dims = (chips, rows, mem, dim, hc, c)
        wq2, wk2, wv2 = (w.reshape(dim, inner) for w in (wq, wk, wv))
        wo2 = wo.reshape(inner, dim)
        gain1 = norm_attn.astype(F32)
        gain2 = norm_mlp.astype(F32)

        pos = (lax.axis_index('seq') // 2) * 2 * mem + jnp.arange(2 * mem)
        bias = jnp.where(pos < mem_len[0], 0.0, -1e30).astype(F32)
        lane = jnp.arange(128)
        ak = jnp.where(lane[None, :] == 0, bias[:, None], jnp.where(lane[None, :] < 4, 1.0, 0.0)).astype(BF16)
        own, att_t, k_c, v_c, kt_c, qz, mem_p, y_all = fwd_call(dims, dec_in, memory, ak, wq2, wk2, wv2, gain1[None, :])
        y_all = y_all.reshape(queries, dim)
        attended = att_t.T

        x_in = dec_in.astype(F32)
        hidden = (x_in + mm(attended, wo2)).astype(BF16)
        n2_f, n2_pull = jax.vjp(rms_norm, hidden.astype(F32), gain2)
        n2 = n2_f.astype(BF16)
        gate_pre = mm(n2, w_gate)
        up_pre = mm(n2, w_up)
        _, gated_pull = jax.vjp(gated_unit, gate_pre, up_pre)
        go_b = grad_out.astype(BF16)
        grad_act = mm_bt(go_b, w_down)
        grad_gate, grad_up = gated_pull(grad_act)
        grad_n2 = mm_bt(grad_gate.astype(BF16), w_gate) + mm_bt(grad_up.astype(BF16), w_up)
        grad_h_norm, g_norm_mlp_part = n2_pull(grad_n2)
        grad_hidden = grad_out + grad_h_norm
        dh = grad_hidden.astype(BF16)
        gn = g_norm_mlp_part.reshape(-1, 2 * rows)
        gn = jnp.concatenate([gn, jnp.zeros((8 - gn.shape[0], 2 * rows), F32)], axis=0)

        g_mem, g_wkv, g_wq, gvec, dq_own, att_all, go_all, dh_all = bwd_call(
            dims, dh, own, gn, attended, go_b, k_c, v_c, kt_c, qz, ak, memory, mem_p, y_all, wo2, wq2, wk2, wv2, gain1[None, :])
        att_all, go_all, dh_all = (t.reshape(queries, dim) for t in (att_all, go_all, dh_all))
        _, norm_pull = jax.vjp(rms_norm, x_in, gain1)
        grad_x_norm, _ = norm_pull(mm_bt(dq_own.T, wq2))
        g_dec = grad_hidden + grad_x_norm

        x_all = y_all.astype(F32)
        g_wo = mm_at(att_all, dh_all)
        h_all = (x_all + mm(att_all, wo2)).astype(BF16)
        n2_all = rms_norm(h_all.astype(F32), gain2).astype(BF16)
        mlp_f, pull_all = jax.vjp(gated_unit, mm(n2_all, w_gate), mm(n2_all, w_up))
        gg, gu = pull_all(mm_bt(go_all, w_down))
        g_down = mm_at(mlp_f.astype(BF16), go_all)
        g_gate = mm_at(n2_all, gg.astype(BF16))
        g_up = mm_at(n2_all, gu.astype(BF16))
        cube = (dim, heads, hd)
        g_wkv = g_wkv.reshape(hc, 2, 128, dim)
        return (g_dec, g_mem, gvec[0], g_wq.reshape(inner, dim).T.reshape(cube), g_wkv[:, 0].reshape(inner, dim).T.reshape(cube),
                g_wkv[:, 1].reshape(inner, dim).T.reshape(cube), g_wo.reshape(heads, hd, dim), gvec[1], g_gate, g_up, g_down)

    return jax.shard_map(device_step, mesh=mesh,
                         in_specs=(row_spec, row_spec, part_vec, row_spec) + (P(),) * 9,
                         out_specs=(row_spec, row_spec, part_vec, part_cube, part_cube, part_cube, part_cube, part_vec, part_mat, part_mat, part_mat),
                         check_vma=False)
```

time: 879 us -> 441 us (0.50)
  waiting for transfers between devices: 474 us -> 0 us
  Pallas kernels: 0 us -> 283 us
  matrix products: 268 us -> 120 us
  blocking collectives: 43.9 us -> 0 us
  other arithmetic: 37.8 us -> 5.42 us
  between operations: 15.4 us -> 1.99 us
  starting transfers between devices: 9.69 us -> 0 us
    pallas_call x0 -> x2, Pallas kernels: none -> 283 us  [the longest x1 193 us: bwd_call(): pl.pallas_call(functools.partial(bwd_kernel, dims), out_shape=(S((mem, di...]
    psum x1 -> x0, waiting for transfers between devices: 274 us -> none  [device_step(): lax.psum((g_norm_attn, g_wq, g_wk, g_wv, g_wo, g_norm_mlp, g_gate, g_up,...]
    dot_general x22 -> x14, matrix products: 256 us -> 120 us  [the longest x4 63.6 us: mm_at(): lax.dot_general(a, b, (((0,), (0,)), ((), ())), preferred_element_type=F32)]
    reduce_scatter x3 -> x0, waiting for transfers between devices: 79.7 us -> none  [the longest x1 64.7 us: device_step(): lax.psum_scatter(local_out * rescale[..., None], 'seq', scatter_dimension...]
    pmax x1 -> x0, waiting for transfers between devices: 70.6 us -> none  [device_step(): global_max = lax.pmax(local_max, 'seq')]
    all_gather x2 -> x0, waiting for transfers between devices: 49.4 us -> none  [the longest x1 37.5 us: device_step(): lax.all_gather(local_query, 'seq', axis=0, tiled=True)]
    reduce_sum x2 -> x0, other arithmetic: 32.6 us -> none  [the longest x1 31.4 us: device_step(): local_sum = jnp.sum(exp_scores, axis=-1)]
    psum x1 -> x0, blocking collectives: 24.8 us -> none  [device_step(): lax.psum((g_norm_attn, g_wq, g_wk, g_wv, g_wo, g_norm_mlp, g_gate, g_up,...]
  transfers between devices with their start and end apart: 7 -> 0, of which waited for: 6 -> 0; matrix products, arithmetic and copies ran while one was open for 19% -> 0% of each run, Pallas kernels for 0% -> 0%
where the time goes in v3:
time: 441 us; the launch traced here: 434 us
  Pallas kernels  283 us (64%)
  matrix products  120 us (27%)
  local copies, waits for them, and re-layouts  22.8 us (5%)
  other arithmetic  5.42 us (1%)
    pallas_call x1, Pallas kernels, bwd_call(): pl.pallas_call(functools.partial(bwd_kernel, dims), out_shape=(S((mem, di...  193 us
    pallas_call x1, Pallas kernels, fwd_call(): pl.pallas_call(functools.partial(fwd_kernel, dims), out_shape=(S((inner +...  90.3 us
    dot_general x4, matrix products, mm_at(): lax.dot_general(a, b, (((0,), (0,)), ((), ())), preferred_element_type=F32)  63.6 us
    dot_general x5, matrix products, mm(): return jnp.dot(a, b, preferred_element_type=F32)  33.3 us
    dot_general x5, matrix products, mm_bt(): lax.dot_general(a, b, (((1,), (1,)), ((), ())), preferred_element_type=F32)  23.4 us

profile of v3, /device:TPU:21, one launch (start us, length us, event | category | flops | bytes accessed | tf_op | source)
XLA Modules:
  0.0 433.7 jit_solution(2400229210496390099)
XLA Ops:
  6.2 4.1 fusion.43
  10.3 1.4 copy.30.wq_ref
  11.8 1.4 copy.31.wk_ref
  13.2 1.4 copy.32.wv_ref
  14.7 90.3 %attn_fwd.1 = (f32[392,256]{1,0:T(8,128)}, bf16[768,128]{1,0:T(8,128)(2,1)}, bf16[2048,384]{1,0:T(8,128)(2,1)}, bf16[2048,384]{1,0:T(8,128)(2,1)}, bf16[384,2048...) custom-call(bf16[128,768]{1,0:T(8,128)(2,1)} %y_ref.1, ...), custom_call_target="tpu_custom_call" | custom-call | flops 10000000000 | bytes 31457280 | tf_op jit(solution)/shard_map/attn_fwd/pallas_call | solution.py:726
  105.0 1.7 copy.33
  106.7 1.9 multiply_reduce_fusion.2
  108.7 3.5 fusion.33
  112.2 5.1 %fusion.18 = f32[128,768]{1,0:T(8,128)} fusion(bf16[768,2048]{1,0:T(8,128)(2,1)S(1)} %copy-done.3, f32[128,2048]{1,0:T(8,128)} %fusion.33, f32[128,2048]{1,0:T(8,128)} %fusion.43, bf16[768,2048]{1,0:T(8,128)(2,1)} %param.24, f32[128,768]{1,0:T(8,128)S(1)} %get-tuple-element.56, f32[768]{0:T(1024)S(1)} %convert_element_type.60, f32[128]{0:T(128)S(1)} %fusion.26), kind=kOutput, calls=%fused_computation.28 | convolution fusion | flops 808484864 | bytes 9178624 | tf_op jit(solution)/shard_map/dot_general | solution.py:23
  117.3 3.9 multiply_reduce_fusion
  122.8 192.9 %attn_bwd.1 = (f32[1024,768]{1,0:T(8,128)}, f32[2,3,8,2,16,768]{5,4,3,2,1,0:T(8,128)}, f32[2,384,768]{2,1,0:T(8,128)}, f32[2,768]{1,0:T(2,128)}, bf16[768,128]{1...) custom-call(bf16[128,768]{1,0:T(8,128)(2,1)} %get-tuple-element.49.d, ...), custom_call_target="tpu_custom_call" | custom-call | flops 10000000000 | bytes 31457280 | tf_op jit(solution)/shard_map/attn_bwd/pallas_call | solution.py:533
  317.1 8.0 %fusion.8 = (f32[2048]{0:T(1024)S(1)}, bf16[2048,768]{1,0:T(8,128)(2,1)}) fusion(bf16[2048,768]{1,0:T(8,128)(2,1)} %bitcast.56, bf16[768,768]{1,0:T(8,128)(2,1)} %bitcast.66, bf16[2048,768]{1,0:T(8,128)(2,1)} %bitcast.69), kind=kOutput, calls=%fused_computation.13 | convolution fusion | flops 2425354240 | bytes 10625024 | tf_op jit(solution)/shard_map/dot_general | solution.py:19
  326.5 4.7 %copy.37 = bf16[768,2048]{1,0:T(8,128)(2,1)} copy(bf16[768,2048]{0,1:T(8,128)(2,1)} %bitcast.57) | data formatting | bytes 6291456 | tf_op jit(solution)/shard_map/dot_general | solution.py:27
  331.2 7.0 %fusion.44 = f32[12,64,768]{2,1,0:T(8,128)} fusion(bf16[12,64,2048]{2,1,0:T(8,128)(2,1)} %bitcast.58, bf16[2048,768,1]{1,0,2:T(8,128)(2,1)} %bitcast.72), kind=kOutput, calls=%fused_computation.70 | convolution fusion | flops 2415919104 | bytes 8650752 | tf_op jit(solution)/shard_map/dot_general | solution.py:27
  338.2 3.0 fusion.42
  341.2 1.6 copy-done.16
  342.8 10.0 %fusion.36 = f32[2048,2048]{1,0:T(8,128)} fusion(bf16[768,2048]{1,0:T(8,128)(2,1)S(1)} %copy-done.4, bf16[2048,768]{1,0:T(8,128)(2,1)S(1)} %copy-done.16, f32[768]{0:T(1024)S(1)} %convert_element_type.60, f32[2048]{0:T(1024)S(1)} %add_rsqrt_fusion), kind=kOutput, calls=%fused_computation.65 | convolution fusion | flops 6448742400 | bytes 23079936 | tf_op jit(solution)/shard_map/dot_general | solution.py:19
  352.7 9.9 %fusion.38 = f32[2048,2048]{1,0:T(8,128)} fusion(bf16[768,2048]{1,0:T(8,128)(2,1)S(1)} %copy-done.14, bf16[2048,768]{1,0:T(8,128)(2,1)S(1)} %copy-done.16, f32[768]{0:T(1024)S(1)} %convert_element_type.60, f32[2048]{0:T(1024)S(1)} %add_rsqrt_fusion), kind=kOutput, calls=%fused_computation.66 | convolution fusion | flops 6448742400 | bytes 23079936 | tf_op jit(solution)/shard_map/dot_general | solution.py:19
  362.7 16.6 %fusion.5 = f32[2048,768]{1,0:T(8,128)} fusion(bf16[2048,768]{1,0:T(8,128)(2,1)S(1)} %bitcast.70, f32[2048,2048]{1,0:T(8,128)} %fusion.38, f32[2048,2048]{1,0:T(8,128)} %fusion.36), kind=kOutput, calls=%fused_computation.9 | convolution fusion | flops 6467616768 | bytes 42991616 | tf_op jit(solution)/shard_map/dot_general | solution.py:27
  379.2 9.8 %fusion.45 = f32[2048,2048]{1,0:T(8,128)} fusion(bf16[2048,768]{1,0:T(8,128)(2,1)S(1)} %bitcast.71, bf16[2048,768]{1,0:T(8,128)(2,1)S(1)} %copy-done.5), kind=kOutput, calls=%fused_computation.71 | convolution fusion | flops 6442450944 | bytes 23068672 | tf_op jit(solution)/shard_map/dot_general | solution.py:23
  389.1 22.9 %fusion.6 = f32[768,2048]{1,0:T(8,128)} fusion(f32[2048,2048]{1,0:T(8,128)} %fusion.36, f32[2048,2048]{1,0:T(8,128)} %fusion.45, f32[2048,2048]{1,0:T(8,128)} %fusion.38, bf16[2048,768]{1,0:T(8,128)(2,1)} %get-tuple-element.60, f32[768]{0:T(1024)S(1)} %convert_element_type.60, f32[2048]{0:T(1024)S(1)} %add_rsqrt_fusion), kind=kOutput, calls=%fused_computation.10 | convolution fusion | flops 6494879744 | bytes 59780096 | tf_op jit(solution)/shard_map/dot_general | solution.py:27
  411.9 17.1 %fusion.4 = f32[768,2048]{1,0:T(8,128)} fusion(f32[2048,2048]{1,0:T(8,128)} %fusion.45, f32[2048,2048]{1,0:T(8,128)} %fusion.36, bf16[2048,768]{1,0:T(8,128)(2,1)} %get-tuple-element.60, f32[768]{0:T(1024)S(1)} %convert_element_type.60, f32[2048]{0:T(1024)S(1)} %add_rsqrt_fusion), kind=kOutput, calls=%fused_computation.8 | convolution fusion | flops 6473908224 | bytes 43002880 | tf_op jit(solution)/shard_map/dot_general | solution.py:27
  429.1 1.7 copy.43
  431.9 1.4 copy.44
  (56 shorter events, 10.3 us)
Async XLA Ops:
  0.6 9.7 %copy-start = (bf16[768,12,64]{0,2,1:T(8,128)(2,1)S(1)}, bf16[768,12,64]{0,2,1:T(8,128)(2,1)}, u32[]{:S(2)}) copy-start(bf16[768,12,64]{0,2,1:T(8,128)(2,1)} %param.18) | copy-start | bytes 3538948
  5.1 1.1 copy-start.12
  6.2 5.5 %copy-start.10 = (bf16[768,12,64]{0,2,1:T(8,128)(2,1)S(1)}, bf16[768,12,64]{0,2,1:T(8,128)(2,1)}, u32[]{:S(2)}) copy-start(bf16[768,12,64]{0,2,1:T(8,128)(2,1)} %param.19) | copy-start | bytes 3538948
  10.3 2.9 copy-start.11
  106.7 5.5 %copy-start.3 = (bf16[768,2048]{1,0:T(8,128)(2,1)S(1)}, bf16[768,2048]{1,0:T(8,128)(2,1)}, u32[]{:S(2)}) copy-start(bf16[768,2048]{1,0:T(8,128)(2,1)} %param.23) | copy-start | bytes 9437188
  117.3 3.9 copy-start.8
  317.1 8.0 %copy-start.1 = (bf16[768,12,64]{0,2,1:T(8,128)(2,1)S(1)}, bf16[768,12,64]{0,2,1:T(8,128)(2,1)}, u32[]{:S(2)}) copy-start(bf16[768,12,64]{0,2,1:T(8,128)(2,1)} %param.18) | copy-start | bytes 3538948
  317.1 8.0 %copy-start.7 = (bf16[128,768]{1,0:T(8,128)(2,1)S(1)}, bf16[128,768]{1,0:T(8,128)(2,1)}, u32[]{:S(2)}) copy-start(bf16[128,768]{1,0:T(8,128)(2,1)} %y_ref.1) | copy-start | bytes 589828
  317.1 8.1 %copy-start.13 = (bf16[768,128]{1,0:T(8,128)(2,1)S(1)}, bf16[768,128]{1,0:T(8,128)(2,1)}, u32[]{:S(2)}) copy-start(bf16[768,128]{1,0:T(8,128)(2,1)} %get-tuple-element.35) | copy-start | bytes 589828
  317.1 8.5 %copy-start.9 = (f32[128,768]{1,0:T(8,128)S(1)}, f32[128,768]{1,0:T(8,128)}, u32[]{:S(2)}) copy-start(f32[128,768]{1,0:T(8,128)} %get-tuple-element.50) | copy-start | bytes 1179652
  326.5 11.7 %slice-start = ((s8[4718592]{0:T(1024)(128)(4,1)}), s8[524288]{0:T(1024)(128)(4,1)S(1)}, s32[]{:S(2)}) async-start(s8[4718592]{0:T(1024)(128)(4,1)} %bitcast.51), calls=%async_computation | async-start | bytes 1048576
  331.2 7.0 %slice-start.1 = ((s8[4718592]{0:T(1024)(128)(4,1)}), s8[4194304]{0:T(1024)(128)(4,1)S(1)}, s32[]{:S(2)}) async-start(s8[4718592]{0:T(1024)(128)(4,1)} %bitcast.51), calls=%async_computation.1 | async-start | bytes 8388608
  338.2 3.0 copy-start.4
  338.2 4.5 %copy-start.16 = (bf16[2048,768]{1,0:T(8,128)(2,1)S(1)}, bf16[2048,768]{1,0:T(8,128)(2,1)}, u32[]{:S(2)}) copy-start(bf16[2048,768]{1,0:T(8,128)(2,1)} %get-tuple-element.60) | copy-start | bytes 9437188
  342.8 10.0 %copy-start.14 = (bf16[768,2048]{1,0:T(8,128)(2,1)S(1)}, bf16[768,2048]{1,0:T(8,128)(2,1)}, u32[]{:S(2)}) copy-start(bf16[768,2048]{1,0:T(8,128)(2,1)} %param.24) | copy-start | bytes 9437188
  352.7 9.9 %copy-start.15 = (bf16[8,2,2,64,768]{4,3,2,1,0:T(8,128)(2,1)S(1)}, bf16[8,2,2,64,768]{4,3,2,1,0:T(8,128)(2,1)}, u32[]{:S(2)}) copy-start(bf16[8,2,2,64,768]{4,3,2,1,0:T(8,128)(2,1)} %get-tuple-element.42) | copy-start | bytes 9437188
  362.6 16.6 %copy-start.5 = (bf16[2048,768]{1,0:T(8,128)(2,1)S(1)}, bf16[2048,768]{1,0:T(8,128)(2,1)}, u32[]{:S(2)}) copy-start(bf16[2048,768]{1,0:T(8,128)(2,1)} %param.25) | copy-start | bytes 9437188
  411.9 17.1 %copy-start.2 = (f32[1024,768]{1,0:T(8,128)S(1)}, f32[1024,768]{1,0:T(8,128)}, u32[]{:S(2)}) copy-start(f32[1024,768]{1,0:T(8,128)} %get-tuple-element.73) | copy-start | bytes 9437188
  429.1 2.8 copy-start.6

commit v4 on v3

--- a/solution.py
+++ b/solution.py
@@ -211,11 +211,13 @@
     return hi, mid, lo
 
 
-def bwd_kernel(dims, dh_ref, own_ref, gn_ref, att_ref, go_ref, k_ref, v_ref, kt_ref, qz_ref, ak_ref, ma_ref, mb_ref, y_ref, wo_ref, wq_ref, wk_ref, wv_ref, g1_ref,
-               gmem_ref, gwkv_ref, gwq_ref, gvec_ref, dqo_ref, attg, gog, dho,
+def bwd_kernel(dims, dh_ref, own_ref, gn_ref, att_ref, go_ref, k_ref, v_ref, kt_ref, qz_ref, ak_ref, wo_ref, wq_ref, wk_ref, wv_ref, g1_ref, g2_ref,
+               ma_hbm, mb_hbm, y_hbm, wg_hbm, wu_hbm, wd_hbm,
+               gvec_ref, dqo_ref, gmem, gwkv, gwq, gwo, gdown, ggate, gup, attg, gog,
                dhg, doz, aqs, ads, stb, dk, dv, dkv, dkvp, dqp, dqr, dqa, arp, arr, ara, pvec, pdq, spb,
+               msc, ybuf, abuf, wbuf, dbuf, wt, gst, gwo_s, gwq_s,
                *sems):
-    chips, rows, mem, dim, hc, c = dims
+    chips, rows, mem, dim, hc, c, ff = dims
     QT = 2 * rows
     T = 2 * mem
     MC = min(256, mem)
@@ -223,6 +225,9 @@
     inner = hc * 64
     np_ = hc // 2
     seg = 256 // chips // 2
+    fh = ff // 2
+    FT = wt.shape[1]
+    nf = fh // FT
     ring = Ring(chips)
     z, core, far = ring.z, ring.core, ring.far
     sems = list(sems)
@@ -242,27 +247,39 @@
     dq_s = [Share(ring, dqa.at[p], lambda half, p=p: dqa.at[p, z, half], take(2)) for p in range(np_)]
     ar_r = [Reduce(ring, arp.at[p], arr.at[p], add_into, take(2)) for p in range(np_)]
     ar_s = [Share(ring, ara.at[p], lambda half, p=p: ara.at[p, z, half], take(2)) for p in range(np_)]
-    xs, xr, ls = take(3)
+    xs, xr, ls, gs, gr, gl, wsem, ysem = take(8)
+    part_ = functools.partial
     ring.enter()
     dh_g.start()
     locals_ = []
+
+    def local(src, dst, n):
+        cp = pltpu.make_async_copy(src, dst, ls.at[n])
+        cp.start()
+        locals_.append(cp)
+        return cp
+
     for n, (ref, buf) in enumerate(((att_ref, attg), (go_ref, gog))):
         for half in range(2):
-            cp = pltpu.make_async_copy(ref.at[pl.ds(half * half_rows, half_rows)], buf.at[z, core, half], ls.at[2 * n + half])
-            cp.start()
-            locals_.append(cp)
+            local(ref.at[pl.ds(half * half_rows, half_rows)], buf.at[z, core, half], 2 * n + half)
+    m_loads = [pltpu.make_async_copy(src, msc.at[n, pl.ds(0, mem)], ls.at[4 + n]) for n, src in enumerate((ma_hbm, mb_hbm))]
+    for cp in m_loads:
+        cp.start()
     for half in range(2):
         dhg[z, core, half] = dh_ref[half * half_rows:(half + 1) * half_rows, :]
     doz[...] = jnp.zeros_like(doz)
     hrow = pl.ds(pl.multiple_of(core * inner, inner), inner)
-    orow = pl.ds(pl.multiple_of((1 - core) * inner, inner), inner)
-    wo_h = wo_ref[hrow, :]
-
-    def d_out(chip):
-        return mm_bt(wo_h, dhg[chip].reshape(QT, dim))
+    hcol = pl.ds(pl.multiple_of(core * inner, 128), inner)
+    other_cols = pl.ds(pl.multiple_of((1 - core) * mem, mem), mem)
+    my_cols = pl.ds(pl.multiple_of(core * mem, mem), mem)
+    qmine = pl.ds(pl.multiple_of(core * rows, rows), rows)
+    qother = pl.ds(pl.multiple_of((1 - core) * rows, rows), rows)
 
     def lanes(chip):
         return pl.ds(pl.multiple_of(chip * QT, QT), QT)
+
+    def d_out(chip):
+        return mm_bt(wo_ref[hrow, :], dhg[chip].reshape(QT, dim))
 
     def prepare(chip, dot=None):
         dot = d_out(chip) if dot is None else dot
@@ -326,38 +343,43 @@
     far_first = [far] + [s * o for o in range(far - 1, 0, -1) for s in (1, -1)] + [0]
     scale = 0.125
 
+    def xp(p):
+        return remote(dkv.at[p, :, other_cols], dkvp.at[p], xs.at[p], xr.at[p], ring.partner)
+
+    def xq(p):
+        return remote(dqa.at[p, z, :, :, qother], pdq.at[p], xs.at[np_ + p], xr.at[np_ + p], ring.partner)
+
+    def at(i, events):
+        for kk, fns in sorted(events.items()):
+            def run(fns=fns):
+                for f in fns:
+                    f()
+            pl.when(i == kk)(run)
+
     def run_pair(p, order, before, after):
         dk[...] = jnp.zeros_like(dk)
         dv[...] = jnp.zeros_like(dv)
 
         def body(i, carry):
             chip = ring.chip(pick(i, order))
-            for kk, fn in sorted(before.items()):
-                pl.when(i == kk)(functools.partial(fn, chip))
+            at(i, {kk: [part_(fn, chip)] for kk, fn in before.items()})
             lax.fori_loop(0, 2, lambda hl, cc: (tile(2 * p + hl, chip, p, hl), cc)[1], 0)
-            for kk, fn in sorted(after.items()):
-                pl.when(i == kk)(fn)
+            at(i, after)
             return carry
 
         lax.fori_loop(0, chips, body, 0)
-        dkb = (dk[...] * scale).astype(BF16)
-        dvb = dv[...].astype(BF16)
-        dkv[p, 0:128, :] = dkb
-        dkv[p, 128:256, :] = dvb
+        dkv[p, 0:128, :] = (dk[...] * scale).astype(BF16)
+        dkv[p, 128:256, :] = dv[...].astype(BF16)
         xp(p).start()
+        if p == 0:
+            for cp in m_loads:
+                cp.wait()
         for part in range(2):
-            mine = pl.ds(pl.multiple_of(core * mem, mem), mem)
-            other = pl.ds(pl.multiple_of((1 - core) * mem, mem), mem)
-            g = mm(dkv[p, part * 128:(part + 1) * 128, mine], ma_ref[...]) + mm(dkv[p, part * 128:(part + 1) * 128, other], mb_ref[...])
+            e = slice(part * 128, (part + 1) * 128)
+            g = mm(dkv[p, e, my_cols], msc[0, 0:mem]) + mm(dkv[p, e, other_cols], msc[1, 0:mem])
             for n in range(128 // seg):
                 row = part * 128 + n * seg
                 arp[p, row // (2 * seg), (row // seg) % 2] = g[n * seg:(n + 1) * seg]
-
-    other_cols = pl.ds(pl.multiple_of((1 - core) * mem, mem), mem)
-    my_cols = pl.ds(pl.multiple_of(core * mem, mem), mem)
-
-    def xp(p):
-        return remote(dkv.at[p, :, other_cols], dkvp.at[p], xs.at[p], xr.at[p], ring.partner)
 
     def gate(off, t=None):
         def fn(chip):
@@ -374,52 +396,40 @@
             before0[n] = gate(off, abs(off) if off > 0 else None)
     run_pair(0, near, before0, {})
 
-    def seq(*fns):
-        def run(*_):
-            for f in fns:
-                f()
-        return run
-
-    part_ = functools.partial
-    def bg_reduce(p, base):
-        ev = {}
-        for n, o in enumerate(range(far, 0, -1)):
-            ev.setdefault(2 * n, []).extend([part_(dq_r[p].both, o), part_(ar_r[p].both, o)])
-        return ev
-
-    def finish_reduce(p):
+    def reduce_events(p):
+        return {2 * n: [part_(dq_r[p].both, o), part_(ar_r[p].both, o)] for n, o in enumerate(range(far, 0, -1))}
+
+    def share_dq(p):
+        for half in range(2):
+            dqa[p, z, half] = (dqp[p, z, half] * scale).astype(BF16)
+        dq_s[p].start()
+        xq(p).start()
+
+    def share_ar(p):
+        for half in range(2):
+            ara[p, z, half] = arp[p, z, half]
+        ar_s[p].start()
+
+    def finish(p):
         dq_r[p].final()
         ar_r[p].final()
-        for half in range(2):
-            dqa[p, z, half] = (dqp[p, z, half] * scale).astype(BF16)
-            ara[p, z, half] = arp[p, z, half]
-        dq_s[p].start()
-        ar_s[p].start()
-        xq(p).start()
-
-    qother = pl.ds(pl.multiple_of((1 - core) * rows, rows), rows)
-
-    def xq(p):
-        return remote(dqa.at[p, z, :, :, qother], pdq.at[p], xs.at[np_ + p], xr.at[np_ + p], ring.partner)
+        share_dq(p)
+        share_ar(p)
 
     def merged(*evs):
         out = {}
         for ev in evs:
             for kk, fns in ev.items():
                 out.setdefault(kk, []).extend(fns)
-        return {kk: seq(*fns) for kk, fns in out.items()}
-
-    def spread(g):
-        return {2 * t - 1: [part_(g.serve, t)] for t in range(1, far + 1)}
-
-    cp = pltpu.make_async_copy(dhg, dho, ls.at[4])
-    cp.start()
-    locals_.append(cp)
+        return out
+
+    def spread(g, first):
+        return {2 * t - 2 + first: [part_(g.serve, t)] for t in range(1, far + 1)}
+
     att_g.start()
-    run_pair(1, far_first, {}, merged(bg_reduce(0, 0), spread(att_g)))
-    finish_reduce(0)
+    run_pair(1, far_first, {}, merged(reduce_events(0), spread(att_g, 1)))
+    finish(0)
     go_g.start()
-    tail = {0: [part_(dq_s[0].serve, 1), part_(ar_s[0].serve, 1)], 2: [part_(dq_s[0].serve, 2), part_(ar_s[0].serve, 2)], 4: [part_(dq_s[0].serve, 3), part_(ar_s[0].serve, 3)], 6: [part_(dq_s[0].serve, 4), part_(ar_s[0].serve, 4)]}
     inl = {}
     for n, off in enumerate(far_first):
         if off == far:
@@ -428,23 +438,192 @@
             inl[n] = [part_(dq_r[2].step, RIGHT, off)]
         elif off < 0:
             inl[n] = [part_(dq_r[2].step, LEFT, -off)]
-    run_pair(2, far_first, {}, merged(bg_reduce(1, 0), tail, spread(go_g), inl))
-    finish_reduce(1)
+    run_pair(2, far_first, {}, merged(inl, reduce_events(1), spread(dq_s[0], 0), spread(ar_s[0], 0), spread(go_g, 1)))
     ar_r[2].both(far)
+    finish(1)
     dq_r[2].final()
-    for half in range(2):
-        dqa[2, z, half] = (dqp[2, z, half] * scale).astype(BF16)
-    dq_s[2].start()
-    xq(2).start()
+    share_dq(2)
+
+    for cp in locals_:
+        cp.wait()
+    for off in near:
+        att_g.ready(off)
+    gain2 = g2_ref[...]
+    gwo_s[...] = jnp.zeros_like(gwo_s)
+
+    def y_fetch(ch, slot):
+        return pltpu.make_async_copy(y_hbm.at[ch], ybuf.at[slot], ysem.at[slot, 0])
+
+    def fetch(ch, slot):
+        return (y_fetch(ch, slot), pltpu.make_async_copy(attg.at[ch], abuf.at[slot], ysem.at[slot, 1]))
+
+    def n2_at(ch):
+        nh = chips // 2
+        return ch // nh, pl.ds(pl.multiple_of((ch - nh * (ch // nh)) * QT, QT), QT)
+
+    for cp in fetch(0, 0):
+        cp.start()
+
+    def hidden(ch, carry):
+        slot = ch % 2
+        for cp in fetch(ch, slot):
+            cp.wait()
+
+        @pl.when(ch + 1 < chips)
+        def _():
+            for cp in fetch(ch + 1, 1 - slot):
+                cp.start()
+        att = abuf[slot].reshape(QT, dim)
+        h = (ybuf[slot].reshape(QT, dim).astype(F32) + mm(att, wo_ref[...])).astype(BF16)
+        a, b = n2_at(ch)
+        msc[a, b, :] = rms_norm(h.astype(F32), gain2).astype(BF16)
+        ah = jnp.where(core == 0, att[:, :inner], att[:, inner:])
+        gwo_s[...] += mm_at(ah, dhg[ch].reshape(QT, dim))
+        at(ch, {1: [part_(ar_r[2].both, 3), part_(dq_s[1].serve, 1), part_(ar_s[1].serve, 1)],
+                4: [part_(dq_s[2].serve, 1), part_(dq_s[1].serve, 2), part_(ar_s[1].serve, 2), part_(ar_r[2].both, 2)],
+                7: [part_(dq_s[2].serve, 2), part_(dq_s[1].serve, 3), part_(ar_s[1].serve, 3)]})
+        return carry
+
+    lax.fori_loop(0, chips, hidden, 0)
+    for off in near:
+        go_g.ready(off)
+    dh_g.drain()
+    go_load = pltpu.make_async_copy(gog, dhg, ls.at[0])
+    go_load.start()
+
+    def partner_rows(buf, out, first, n, k):
+        dst = out.at[pl.ds(pl.multiple_of(first, n), n)]
+        return pltpu.make_async_copy(buf, dst, gl.at[k]), remote(buf, dst, gs.at[k], gr.at[k], ring.partner)
+
+    def both_start(pair):
+        pair[0].start()
+        pair[1].start()
+
+    def both_wait(pair):
+        pair[0].wait()
+        pair[1].wait()
+
+    wo_out = partner_rows(gwo_s, gwo, core * inner, inner, 3 * nf)
+    both_start(wo_out)
+
+    def w_fetch(f, slot):
+        cols = pl.ds(pl.multiple_of(core * fh + f * FT, FT), FT)
+        return (pltpu.make_async_copy(wg_hbm.at[:, cols], wbuf.at[slot, 0], wsem.at[slot, 0]),
+                pltpu.make_async_copy(wu_hbm.at[:, cols], wbuf.at[slot, 1], wsem.at[slot, 1]),
+                pltpu.make_async_copy(wd_hbm.at[cols], dbuf.at[slot], wsem.at[slot, 2]))
+
+    for cp in w_fetch(0, 0):
+        cp.start()
+    go_load.wait()
+    f_events = {0: [part_(ar_r[2].both, 1), part_(dq_s[2].serve, 3), part_(dq_s[1].serve, 4), part_(ar_s[1].serve, 4)],
+                1: [ar_r[2].final, part_(share_ar, 2), part_(dq_s[2].serve, 4)]}
+    f_events2 = {2: [part_(ar_s[2].serve, 1), part_(ar_s[2].serve, 2)],
+                 3: [part_(ar_s[2].serve, 3), part_(ar_s[2].serve, 4)]}
+    outs3 = (gdown, ggate, gup)
+
+    def mlp(f, carry):
+        slot = f % 2
+        for cp in w_fetch(f, slot):
+            cp.wait()
+
+        @pl.when(f + 1 < nf)
+        def _():
+            for cp in w_fetch(f + 1, 1 - slot):
+                cp.start()
+        for n in range(2):
+            wt[n] = wbuf[slot, n].T
+
+        def act_chunk(ch, cc):
+            a, b = n2_at(ch)
+            n2 = msc[a, b, :]
+            g = mm_bt(wt[0], n2)
+            u = mm_bt(wt[1], n2)
+            ga = mm_bt(dbuf[slot], dhg[ch].reshape(QT, dim))
+            sig = jax.nn.sigmoid(g)
+            si = g * sig
+            q = lanes(ch)
+            doz[0:FT, q] = (si * u).astype(BF16)
+            doz[FT:2 * FT, q] = (ga * u * (sig + si * (1.0 - sig))).astype(BF16)
+            doz[2 * FT:3 * FT, q] = (ga * si).astype(BF16)
+            return cc
+
+        lax.fori_loop(0, chips, act_chunk, 0)
+        at(f, f_events)
+        for n in range(3):
+            @pl.when(f > 0)
+            def _(n=n):
+                both_wait(partner_rows(gst.at[n, pl.ds(0, FT)], outs3[n], core * fh + (f - 1) * FT, FT, n * nf + f - 1))
+            acc = None
+            for ch in range(chips):
+                if n == 0:
+                    rhs = dhg[ch].reshape(QT, dim)
+                else:
+                    nh = chips // 2
+                    rhs = msc[ch // nh, (ch % nh) * QT:(ch % nh + 1) * QT, :]
+                d = mm(doz[n * FT:(n + 1) * FT, ch * QT:(ch + 1) * QT], rhs)
+                acc = d if acc is None else acc + d
+            gst[n, 0:FT] = acc
+            both_start(partner_rows(gst.at[n, pl.ds(0, FT)], outs3[n], core * fh + f * FT, FT, n * nf + f))
+        at(f, f_events2)
+        return carry
+
+    lax.fori_loop(0, nf, mlp, 0)
+    for p in range(np_):
+        local(ara.at[p], gwkv.at[core, p], 1 + p)
+    cw = [remote(ara.at[p], gwkv.at[core, p], xs.at[2 * np_ + 2 + p], xr.at[2 * np_ + 2 + p], ring.partner) for p in range(np_)]
+    for p in range(np_):
+        cw[p].start()
+
+    gain = g1_ref[...]
+    wqt = wq_ref[:, hcol].T
+    y_fetch(0, 0).start()
+    spb[...] = jnp.zeros_like(spb)
+
+    def query(ch, carry):
+        slot = ch % 2
+        y_fetch(ch, slot).wait()
+
+        @pl.when(ch + 1 < chips)
+        def _():
+            y_fetch(ch + 1, 1 - slot).start()
+        x = ybuf[slot].reshape(QT, dim).astype(F32)
+        xhat = x * lax.rsqrt(jnp.mean(x * x, axis=-1, keepdims=True) + 1e-6)
+        n1 = (xhat * gain).astype(BF16)
+        dqc = jnp.concatenate([dqa[p, ch].reshape(128, QT) for p in range(np_)], axis=0)
+        dn = mm_at(dqc, wqt)
+        d = mm(dqc, n1)
+
+        @pl.when(ch == 0)
+        def _():
+            gwq_s[...] = d
+
+        @pl.when(ch > 0)
+        def _():
+            gwq_s[...] += d
+        spb[0:1, :] += jnp.sum(dn * xhat, axis=0, keepdims=True)
+        return carry
+
+    lax.fori_loop(0, chips, query, 0)
+    gvec2 = jnp.zeros((16 - 2 * hc, QT), F32)
+    for ch in range(chips):
+        gvec2 = gvec2 + jnp.concatenate([stb[ch, 0, hc:8, :], stb[ch, 1, hc:8, :]], axis=0)
+    for n in range(dim // QT):
+        spb[1:2, n * QT:(n + 1) * QT] = gvec2[n:n + 1]
+    cv = remote(spb, pvec, xs.at[2 * np_], xr.at[2 * np_], ring.partner)
+    cv.start()
+    wq_out = partner_rows(gwq_s, gwq, core * inner, inner, 3 * nf + 1)
+    both_start(wq_out)
+
     for p in range(np_):
         remote(dkvp.at[p], dkvp.at[p], xs.at[p], xr.at[p], ring.partner).wait_recv()
-    step_fns = [[part_(ar_r[2].both, 3), part_(dq_s[1].serve, 1), part_(ar_s[1].serve, 1), part_(dq_s[2].serve, 1)],
-                [part_(ar_r[2].both, 2), part_(dq_s[1].serve, 2), part_(ar_s[1].serve, 2), part_(dq_s[2].serve, 2)],
-                [part_(ar_r[2].both, 1), part_(dq_s[1].serve, 3), part_(ar_s[1].serve, 3), part_(dq_s[2].serve, 3)],
-                [part_(dq_s[1].serve, 4), part_(ar_s[1].serve, 4), part_(dq_s[2].serve, 4)]]
     nb = 4
+    w = mem // nb
+    gm = lambda b: pltpu.make_async_copy(gst.at[b % 3, pl.ds(0, w)], gmem.at[pl.ds(b * w, w)], gl.at[3 * nf + 2 + b % 3])
     for b in range(nb):
-        w = mem // nb
+        if b < 3:
+            both_wait(partner_rows(gst.at[b, pl.ds(0, FT)], outs3[b], core * fh + (nf - 1) * FT, FT, b * nf + nf - 1))
+        else:
+            gm(b - 3).wait()
         cb = pl.ds(pl.multiple_of(core * mem + b * w, w), w)
         acc = None
         for p in range(np_):
@@ -455,74 +634,38 @@
                 d = mm(jnp.concatenate([w_ref[:, own_cols], w_ref[:, oth_cols]], axis=1),
                        jnp.concatenate([dkv[p, e, cb], dkvp[p, e, b * w:(b + 1) * w]], axis=0))
                 acc = d if acc is None else acc + d
-        gmem_ref[b * w:(b + 1) * w, :] = acc.T
-        for f in step_fns[b]:
-            f()
-    ar_r[2].final()
-    for half in range(2):
-        ara[2, z, half] = arp[2, z, half]
-    ar_s[2].start()
-    gain = g1_ref[...]
-    wqt = wq_ref[:, pl.ds(pl.multiple_of(core * inner, 128), inner)].T
-    gvec = jnp.zeros((1, dim), F32)
-    gvec2 = jnp.zeros((16 - 2 * hc, QT), F32)
-    for ch in range(chips):
-        x = y_ref[ch * QT:(ch + 1) * QT, :].astype(F32)
-        xhat = x * lax.rsqrt(jnp.mean(x * x, axis=-1, keepdims=True) + 1e-6)
-        n1 = (xhat * gain).astype(BF16)
-        dqc = jnp.concatenate([dqa[p, ch].reshape(128, QT) for p in range(np_)], axis=0)
-        dn = mm_at(dqc, wqt)
-        d = mm(dqc, n1)
-        if ch == 0:
-            gwq_ref[core] = d
-        else:
-            gwq_ref[core] += d
-        gvec = gvec + jnp.sum(dn * xhat, axis=0, keepdims=True)
-        gvec2 = gvec2 + jnp.concatenate([stb[ch, 0, hc:8, :], stb[ch, 1, hc:8, :]], axis=0)
-        if ch % 2 == 1:
-            ar_s[2].serve(ch // 2 + 1)
-    spb[0:1, :] = gvec
-    for n in range(dim // QT):
-        spb[1:2, n * QT:(n + 1) * QT] = gvec2[n:n + 1]
-    cv = remote(spb, pvec, xs.at[2 * np_], xr.at[2 * np_], ring.partner)
-    cq = remote(gwq_ref.at[core], gwq_ref.at[core], xs.at[2 * np_ + 1], xr.at[2 * np_ + 1], ring.partner)
-    cv.start()
-    cq.start()
-    for p in range(np_):
-        gwkv_ref[core, p] = ara[p]
-    cw = [remote(ara.at[p], gwkv_ref.at[core, p], xs.at[2 * np_ + 2 + p], xr.at[2 * np_ + 2 + p], ring.partner) for p in range(np_)]
-    for p in range(np_):
-        cw[p].start()
-    qmine = pl.ds(pl.multiple_of(core * rows, rows), rows)
+        gst[b % 3, 0:w] = acc.T
+        gm(b).start()
     for p in range(np_):
         own_r = pl.ds(pl.multiple_of(core * inner + p * 128, 128), 128)
         oth_r = pl.ds(pl.multiple_of((1 - core) * inner + p * 128, 128), 128)
         dqo_ref[own_r, :] = dqa[p, z, :, :, qmine].reshape(128, rows)
         xq(p).wait()
         dqo_ref[oth_r, :] = pdq[p].reshape(128, rows)
+        xp(p).wait_send()
     cv.wait()
     gvec_ref[...] = spb[0:2] + pvec[0:2]
-    cq.wait()
+    both_wait(wo_out)
+    both_wait(wq_out)
     for p in range(np_):
         cw[p].wait()
-        xp(p).wait_send()
-    for g in (att_g, go_g):
-        for off in near:
-            g.ready(off)
-    for cp in locals_:
+    for cp in locals_[4:]:
         cp.wait()
-    for obj in [dh_g, att_g, go_g, st_g] + dq_r + dq_s + ar_r + ar_s:
+    for b in range(nb - 3, nb):
+        gm(b).wait()
+    for obj in [att_g, go_g, st_g] + dq_r + dq_s + ar_r + ar_s:
         obj.drain()
 
 
 def bwd_call(dims, *args):
-    chips, rows, mem, dim, hc, c = dims
+    chips, rows, mem, dim, hc, c, ff = dims
     inner = hc * 64
     QT = 2 * rows
     T = 2 * mem
     np_ = hc // 2
     h2 = chips // 2
     seg = 256 // chips // 2
+    FT = ff // 8
     v = pl.BlockSpec(memory_space=VMEM)
     hbm = pl.BlockSpec(memory_space=pl.ANY)
     s3 = (2, 2, h2)
@@ -532,18 +675,22 @@
     gshape = (chips, 2, 2, rows // 2, dim)
     return pl.pallas_call(
         functools.partial(bwd_kernel, dims),
-        out_shape=(S((mem, dim), F32), S((2, np_, chips, 2, seg, dim), F32), S((2, inner, dim), F32), S((2, dim), F32), S((2 * inner, rows), BF16), S(gshape, BF16), S(gshape, BF16), S(gshape, BF16)),
-        in_specs=[v] * 18, out_specs=(v,) * 5 + (hbm,) * 3,
+        out_shape=(S((2, dim), F32), S((2 * inner, rows), BF16), S((mem, dim), F32), S((2, np_, chips, 2, seg, dim), F32), S((2 * inner, dim), F32), S((2 * inner, dim), F32),
+                   S((ff, dim), F32), S((ff, dim), F32), S((ff, dim), F32), S(gshape, BF16), S(gshape, BF16)),
+        in_specs=[v] * 16 + [hbm] * 6, out_specs=(v,) * 2 + (hbm,) * 9,
         scratch_shapes=[
-            VMEM(gshape, BF16), VMEM((hc * 128, chips * QT), BF16), VMEM((hc * 16, chips * QT), BF16), VMEM((hc * 16, chips * QT), BF16),
+            VMEM(gshape, BF16), VMEM((max(hc * 128, 3 * FT), chips * QT), BF16), VMEM((hc * 16, chips * QT), BF16), VMEM((hc * 16, chips * QT), BF16),
             VMEM((chips, 2, 8, QT), F32), VMEM((128, T), F32), VMEM((128, T), F32), VMEM((np_, 256, T), BF16), VMEM((np_, 256, mem), BF16),
             VMEM((np_, chips, 2, 64, QT), F32), VMEM((np_, 2, 2, h2, 64, QT), F32), VMEM((np_, chips, 2, 64, QT), BF16),
             VMEM((np_, chips, 2, seg, dim), F32), VMEM((np_, 2, 2, h2, seg, dim), F32), VMEM((np_, chips, 2, seg, dim), F32),
-            VMEM((8, dim), F32), VMEM((np_, 2, 64, rows), BF16), VMEM((8, dim), F32)]
-        + rows_sems * 3 + two * (1 + 4 * np_) + [DMA((3 * np_ + 2,))] * 2 + [DMA((5,))],
+            VMEM((8, dim), F32), VMEM((np_, 2, 64, rows), BF16), VMEM((8, dim), F32),
+            VMEM((2, max(mem, chips * rows), dim), BF16), VMEM((2, 2, 2, rows // 2, dim), BF16), VMEM((2, 2, 2, rows // 2, dim), BF16),
+            VMEM((2, 2, dim, FT), BF16), VMEM((2, FT, dim), BF16), VMEM((2, FT, dim), BF16), VMEM((3, max(FT, mem // 4), dim), F32), VMEM((inner, dim), F32), VMEM((inner, dim), F32)]
+        + rows_sems * 3 + two * (1 + 4 * np_) + [DMA((3 * np_ + 2,))] * 2 + [DMA((6,)), DMA((14,)), DMA((14,)), DMA((17,)), DMA((2, 3)), DMA((2, 2))],
         compiler_params=pltpu.CompilerParams(vmem_limit_bytes=66_900_000, collective_id=1, has_side_effects=True),
         cost_estimate=pl.CostEstimate(flops=10**10, bytes_accessed=30 << 20, transcendentals=0),
         name="attn_bwd")(*args)
+
 
 def fwd_kernel(dims, y_ref, m_ref, ak_ref, wq_ref, wk_ref, wv_ref, g_ref,
                own, att_ref, k_s, v_s, kt_s, qz, mg, yall,
@@ -748,7 +895,6 @@
         mem = memory.shape[0]
         heads, hd = wq.shape[1], wq.shape[2]
         inner = heads * hd
-        queries = rows * group
         chips = group // 2
         hc = heads // 2
         c = LOG2E * hd ** -0.5
@@ -763,7 +909,6 @@
         lane = jnp.arange(128)
         ak = jnp.where(lane[None, :] == 0, bias[:, None], jnp.where(lane[None, :] < 4, 1.0, 0.0)).astype(BF16)
         own, att_t, k_c, v_c, kt_c, qz, mem_p, y_all = fwd_call(dims, dec_in, memory, ak, wq2, wk2, wv2, gain1[None, :])
-        y_all = y_all.reshape(queries, dim)
         attended = att_t.T
 
         x_in = dec_in.astype(F32)
@@ -783,26 +928,16 @@
         gn = g_norm_mlp_part.reshape(-1, 2 * rows)
         gn = jnp.concatenate([gn, jnp.zeros((8 - gn.shape[0], 2 * rows), F32)], axis=0)
 
-        g_mem, g_wkv, g_wq, gvec, dq_own, att_all, go_all, dh_all = bwd_call(
-            dims, dh, own, gn, attended, go_b, k_c, v_c, kt_c, qz, ak, memory, mem_p, y_all, wo2, wq2, wk2, wv2, gain1[None, :])
-        att_all, go_all, dh_all = (t.reshape(queries, dim) for t in (att_all, go_all, dh_all))
+        gvec, dq_own, g_mem, g_wkv, g_wq, g_wo, g_down, g_gate, g_up, _, _ = bwd_call(
+            dims + (w_gate.shape[1],), dh, own, gn, attended, go_b, k_c, v_c, kt_c, qz, ak, wo2, wq2, wk2, wv2, gain1[None, :], gain2[None, :],
+            memory, mem_p, y_all, w_gate, w_up, w_down)
         _, norm_pull = jax.vjp(rms_norm, x_in, gain1)
         grad_x_norm, _ = norm_pull(mm_bt(dq_own.T, wq2))
         g_dec = grad_hidden + grad_x_norm
-
-        x_all = y_all.astype(F32)
-        g_wo = mm_at(att_all, dh_all)
-        h_all = (x_all + mm(att_all, wo2)).astype(BF16)
-        n2_all = rms_norm(h_all.astype(F32), gain2).astype(BF16)
-        mlp_f, pull_all = jax.vjp(gated_unit, mm(n2_all, w_gate), mm(n2_all, w_up))
-        gg, gu = pull_all(mm_bt(go_all, w_down))
-        g_down = mm_at(mlp_f.astype(BF16), go_all)
-        g_gate = mm_at(n2_all, gg.astype(BF16))
-        g_up = mm_at(n2_all, gu.astype(BF16))
         cube = (dim, heads, hd)
         g_wkv = g_wkv.reshape(hc, 2, 128, dim)
-        return (g_dec, g_mem, gvec[0], g_wq.reshape(inner, dim).T.reshape(cube), g_wkv[:, 0].reshape(inner, dim).T.reshape(cube),
-                g_wkv[:, 1].reshape(inner, dim).T.reshape(cube), g_wo.reshape(heads, hd, dim), gvec[1], g_gate, g_up, g_down)
+        return (g_dec, g_mem, gvec[0], g_wq.T.reshape(cube), g_wkv[:, 0].reshape(inner, dim).T.reshape(cube),
+                g_wkv[:, 1].reshape(inner, dim).T.reshape(cube), g_wo.reshape(heads, hd, dim), gvec[1], g_gate.T, g_up.T, g_down)
 
     return jax.shard_map(device_step, mesh=mesh,
                          in_specs=(row_spec, row_spec, part_vec, row_spec) + (P(),) * 9,

time: 441 us -> 375 us (0.85)
  the two profiles are of different devices: /device:TPU:21 before, /device:TPU:22 now
where the time goes in v4:
time: 375 us; the launch traced here: 368 us
  Pallas kernels  309 us (82%)
  local copies, waits for them, and re-layouts  36.8 us (10%)
  matrix products  16.5 us (4%)
    pallas_call x1, Pallas kernels, bwd_call(): pl.pallas_call(functools.partial(bwd_kernel, dims), out_shape=(S((2, dim)...  220 us
    pallas_call x1, Pallas kernels, fwd_call(): pl.pallas_call(functools.partial(fwd_kernel, dims), out_shape=(S((inner +...  89.1 us
    unnamed x54, local copies, waits for them, and re-layouts  23.3 us
    dot_general x4, matrix products, mm_bt(): lax.dot_general(a, b, (((1,), (1,)), ((), ())), preferred_element_type=F32)  11.5 us

profile of v4, /device:TPU:22, one launch (start us, length us, event | category | flops | bytes accessed | tf_op | source)
XLA Modules:
  0.0 368.0 jit_solution(11259762498440895396)
XLA Ops:
  1.5 1.1 select_convert_fusion.ak_ref
  2.6 2.4 copy.30.wq_ref
  5.0 1.4 copy.31.wk_ref
  6.5 1.4 copy.32.wv_ref
  8.5 89.1 %attn_fwd.1 = (f32[392,256]{1,0:T(8,128)}, bf16[768,128]{1,0:T(8,128)(2,1)}, bf16[2048,384]{1,0:T(8,128)(2,1)}, bf16[2048,384]{1,0:T(8,128)(2,1)}, bf16[384,2048...) custom-call(bf16[128,768]{1,0:T(8,128)(2,1)} %y_ref.1, ...), custom_call_target="tpu_custom_call" | custom-call | flops 10000000000 | bytes 31457280 | tf_op jit(solution)/shard_map/attn_fwd/pallas_call | solution.py:873
  97.7 1.5 multiply_reduce_fusion.2
  99.8 3.5 fusion.17
  103.3 0.7 copy-done.14
  104.0 2.1 fusion.21
  106.1 5.1 %fusion.5 = f32[128,768]{1,0:T(8,128)} fusion(bf16[768,2048]{1,0:T(8,128)(2,1)S(1)} %copy-done.2, f32[128,2048]{1,0:T(8,128)} %fusion.17, f32[128,2048]{1,0:T(8,128)} %fusion.21, bf16[768,2048]{1,0:T(8,128)(2,1)} %wu_hbm.1, f32[128,768]{1,0:T(8,128)S(1)} %get-tuple-element.80, f32[768]{0:T(1024)S(1)} %convert_element_type.39, f32[128]{0:T(128)S(1)} %fusion.13), kind=kOutput, calls=%fused_computation.11 | convolution fusion | flops 808484864 | bytes 9178624 | tf_op jit(solution)/shard_map/dot_general | solution.py:23
  111.1 3.9 %multiply_reduce_fusion = (f32[768]{0:T(1024)S(1)}, f32[128]{0:T(128)S(1)}, f32[128,768]{1,0:T(8,128)S(1)}) fusion(f32[128,768]{1,0:T(8,128)S(1)} %get-tuple-element.80, f32[128]{0:T(128)S(1)} %fusion.13, f32[768]{0:T(1024)S(1)} %convert_element_type.39, f32[128,768]{1,0:T(8,128)} %fusion.5, bf16[768,2048]{1,0:T(8,128)(2,1)} %wu_hbm.1, ...), kind=kOutput, calls=%fused_computation.25 | convolution fusion | flops 404913280 | bytes 6429696 | tf_op jit(solution)/shard_map/dot_general | solution.py:23
  115.1 1.0 fusion.18
  116.6 0.8 copy.33
  118.1 220.3 %attn_bwd.1 = (f32[2,768]{1,0:T(2,128)}, bf16[768,128]{1,0:T(8,128)(2,1)}, f32[1024,768]{1,0:T(8,128)}, f32[2,3,8,2,16,768]{5,4,3,2,1,0:T(8,128)}, f32[768,768]{...) custom-call(bf16[128,768]{1,0:T(8,128)(2,1)} %get-tuple-element.73.d, ...), custom_call_target="tpu_custom_call" | custom-call | flops 10000000000 | bytes 31457280 | tf_op jit(solution)/shard_map/attn_bwd/pallas_call | solution.py:676
  338.4 6.6 %copy.37 = f32[768,2048]{1,0:T(8,128)} copy(f32[768,2048]{0,1:T(8,128)} %bitcast.37) | data formatting | bytes 12582912
  345.0 6.6 %copy.38 = f32[768,2048]{1,0:T(8,128)} copy(f32[768,2048]{0,1:T(8,128)} %bitcast.36) | data formatting | bytes 12582912
  351.5 5.0 %fusion.20 = (f32[6,1,128,768]{3,2,1,0:T(8,128)}, f32[6,1,128,768]{3,2,1,0:T(8,128)}) fusion(f32[6,2,128,768]{3,2,1,0:T(8,128)} %bitcast.38), kind=kLoop, calls=%fused_computation.45 | loop fusion | bytes 9437184 | tf_op jit(solution)/shard_map/slice | solution.py:940
  357.1 0.9 fusion.9
  358.0 0.6 slice_reduce_fusion
  358.6 1.7 copy.44
  360.3 1.4 copy.45
  361.7 1.8 copy-done.4
  363.4 1.4 copy.46
  364.8 2.7 copy.47
  (61 shorter events, 2.9 us)
Async XLA Ops:
  0.6 4.4 %copy-start.11 = (bf16[768,12,64]{0,2,1:T(8,128)(2,1)S(1)}, bf16[768,12,64]{0,2,1:T(8,128)(2,1)}, u32[]{:S(2)}) copy-start(bf16[768,12,64]{0,2,1:T(8,128)(2,1)} %param.19) | copy-start | bytes 3538948
  0.7 5.8 %copy-start.12 = (bf16[768,12,64]{0,2,1:T(8,128)(2,1)S(1)}, bf16[768,12,64]{0,2,1:T(8,128)(2,1)}, u32[]{:S(2)}) copy-start(bf16[768,12,64]{0,2,1:T(8,128)(2,1)} %param.20) | copy-start | bytes 3538948
  2.6 5.3 %copy-start.18 = (bf16[768]{0:T(1024)(128)(2,1)S(1)}, bf16[768]{0:T(1024)(128)(2,1)}, u32[]{:S(2)}) copy-start(bf16[768]{0:T(1024)(128)(2,1)} %param.17) | copy-start | bytes 4612
  8.5 89.2 %copy-start.6 = (bf16[128,768]{1,0:T(8,128)(2,1)S(1)}, bf16[128,768]{1,0:T(8,128)(2,1)}, u32[]{:S(2)}) copy-start(bf16[128,768]{1,0:T(8,128)(2,1)} %y_ref.1) | copy-start | bytes 589828
  8.5 89.2 %copy-start.13 = (bf16[12,64,768]{2,1,0:T(8,128)(2,1)S(1)}, bf16[12,64,768]{2,1,0:T(8,128)(2,1)}, u32[]{:S(2)}) copy-start(bf16[12,64,768]{2,1,0:T(8,128)(2,1)} %param.21) | copy-start | bytes 3538948
  8.5 90.8 %copy-start.17 = (bf16[768]{0:T(1024)(128)(2,1)S(1)}, bf16[768]{0:T(1024)(128)(2,1)}, u32[]{:S(2)}) copy-start(bf16[768]{0:T(1024)(128)(2,1)} %param.22) | copy-start | bytes 4612
  97.7 5.6 %copy-start.8 = (f32[128,768]{1,0:T(8,128)S(1)}, f32[128,768]{1,0:T(8,128)}, u32[]{:S(2)}) copy-start(f32[128,768]{1,0:T(8,128)} %param.16) | copy-start | bytes 1179652
  97.7 6.3 %copy-start.3 = (bf16[2048,768]{1,0:T(8,128)(2,1)S(1)}, bf16[2048,768]{1,0:T(8,128)(2,1)}, u32[]{:S(2)}) copy-start(bf16[2048,768]{1,0:T(8,128)(2,1)} %wd_hbm.1) | copy-start | bytes 9437188
  99.2 0.5 copy-start.20
  103.2 2.8 copy-start.2
  103.3 0.7 copy-start.14
  111.1 3.9 %copy-start.21 = (f32[128]{0:T(128)S(1)}, f32[128]{0:T(128)}, u32[]{:S(2)}) copy-start(f32[128]{0:T(128)} %copy-done.20) | copy-start | bytes 1540
  111.1 3.9 %copy-start.9 = (f32[128,768]{1,0:T(8,128)S(1)}, f32[128,768]{1,0:T(8,128)}, u32[]{:S(2)}) copy-start(f32[128,768]{1,0:T(8,128)} %param.16) | copy-start | bytes 1179652
  111.1 5.5 %copy-start.15 = (bf16[768,128]{1,0:T(8,128)(2,1)S(1)}, bf16[768,128]{1,0:T(8,128)(2,1)}, u32[]{:S(2)}) copy-start(bf16[768,128]{1,0:T(8,128)(2,1)} %get-tuple-element.28) | copy-start | bytes 589828
  351.5 5.0 %copy-start = (bf16[768,12,64]{0,2,1:T(8,128)(2,1)S(1)}, bf16[768,12,64]{0,2,1:T(8,128)(2,1)}, u32[]{:S(2)}) copy-start(bf16[768,12,64]{0,2,1:T(8,128)(2,1)} %param.18) | copy-start | bytes 3538948
  351.5 5.0 %copy-start.7 = (bf16[128,768]{1,0:T(8,128)(2,1)S(1)}, bf16[128,768]{1,0:T(8,128)(2,1)}, u32[]{:S(2)}) copy-start(bf16[128,768]{1,0:T(8,128)(2,1)} %y_ref.1) | copy-start | bytes 589828
  351.5 5.0 %copy-start.16 = (bf16[768,128]{1,0:T(8,128)(2,1)S(1)}, bf16[768,128]{1,0:T(8,128)(2,1)}, u32[]{:S(2)}) copy-start(bf16[768,128]{1,0:T(8,128)(2,1)} %get-tuple-element.36) | copy-start | bytes 589828
  351.5 5.5 %copy-start.10 = (f32[128,768]{1,0:T(8,128)S(1)}, f32[128,768]{1,0:T(8,128)}, u32[]{:S(2)}) copy-start(f32[128,768]{1,0:T(8,128)} %get-tuple-element.74) | copy-start | bytes 1179652
  356.5 1.4 copy-start.19
  356.5 2.0 copy-start.1
  357.0 3.2 copy-start.5
  358.6 6.3 %slice-start = ((s8[6291456]{0:T(1024)(128)(4,1)}), s8[4194304]{0:T(1024)(128)(4,1)S(1)}, s32[]{:S(2)}) async-start(s8[6291456]{0:T(1024)(128)(4,1)} %bitcast.34), calls=%async_computation | async-start | bytes 8388608
  360.2 3.2 copy-start.4
  360.3 4.6 %slice-start.1 = ((s8[6291456]{0:T(1024)(128)(4,1)}), s8[2097152]{0:T(1024)(128)(4,1)S(1)}, s32[]{:S(2)}) async-start(s8[6291456]{0:T(1024)(128)(4,1)} %bitcast.34), calls=%async_computation.1 | async-start | bytes 4194304
